TPU v7x, 256 devices: a whole 4x4x8 slice. The times are simulated.
256 devices in a mesh: gx: 8 (over x, z_lo), gy: 4 (over y), gz: 8 (over z_hi, core).
Axes of the slice: x: 4, y: 4, z: 8 (z_hi: 4, z_lo: 2; z = z_hi * 2 + z_lo), core: 2. Of those that a mesh axis runs over, the one named last changes fastest.
Arguments:
- positions: float32 [3, 262144], P(None, ('gx', 'gy', 'gz')), may hold values from 0 to 32, as said below
- velocities: float32 [3, 262144], P(None, ('gx', 'gy', 'gz')), may hold values from -6 to 6
- inv_mass: float32 [262144], P(('gx', 'gy', 'gz')), may hold values from 0.5 to 2
- charge: float32 [262144], P(('gx', 'gy', 'gz')), may hold values from -4 to 4
- fast_force: float32 [3, 262144], P(None, ('gx', 'gy', 'gz')), may hold values from -6 to 6
- slow_force: float32 [3, 262144], P(None, ('gx', 'gy', 'gz')), may hold values from -6 to 6
- bonds: int32 [2, 262144], P(None, ('gx', 'gy', 'gz')), may hold values from 0 to 1023
- bond_k: float32 [262144], P(('gx', 'gy', 'gz')), may hold values from 0.05 to 0.4
- halo_index: int32 [6, 65536], P(None, ('gx', 'gy', 'gz')), may hold values from 0 to 1023
- pair_own: int32 [49152], P(('gx', 'gy', 'gz')), may hold values from 0 to 7
- pair_partner: int32 [49152], P(('gx', 'gy', 'gz')), may hold values from 0 to 19
- pair_count: int32 [256], P(('gx', 'gy', 'gz')), may hold values from 1 to 192
Outputs:
- displacement: float32 [3, 262144], P(None, ('gx', 'gy', 'gz'))
- velocities_out: float32 [3, 262144], P(None, ('gx', 'gy', 'gz'))
- fast_out: float32 [3, 262144], P(None, ('gx', 'gy', 'gz'))
- slow_out: float32 [3, 262144], P(None, ('gx', 'gy', 'gz'))
Inputs may be any that keep to these rules, and one draw needn't show every extreme that they name: `positions`: atoms of patch p lie in the cube of side 4 at 4 times its grid place.
All inputs are finite; a program needn't handle non-finite values.
Results may differ from a plain program's by a relative error of at most 0.0003.
Values sent between devices are 32-bit elements; how exact they have to be, the bound alone decides.
A program may use at most 64 MiB of HBM per device.

v0:
```python
import math

import jax
import jax.numpy as jnp
from jax import lax
from jax.sharding import Mesh
from jax.sharding import PartitionSpec as P

INNER = 4
GZ = ("gz_0", "gz_1")
GY_GZ = ("gy", "gz_0", "gz_1")
GX_GY_GZ = ("gx", "gy", "gz_0", "gz_1")


step_inner = 0.1
short_scale = 1.0
short_reach = 0.64
long_scale = 0.5
long_reach = 1.44


def padded(block, sides, width):
    for axis, dim in sides:
        count = lax.axis_size(axis)
        forward = [(i, i + 1) for i in range(count - 1)]
        backward = [(target, source) for source, target in forward]
        low = lax.ppermute(
            lax.slice_in_dim(block, block.shape[dim] - width, None, axis=dim), axis, forward
        )
        high = lax.ppermute(lax.slice_in_dim(block, 0, width, axis=dim), axis, backward)
        block = jnp.concatenate([low, block, high], axis=dim)
    return block


def sent_together(arrays, axis, split_dim, concat_dim, along):
    widths = [math.prod(a.shape[along:]) for a in arrays]
    both = jnp.concatenate(
        [a.reshape(*a.shape[:along], w) for a, w in zip(arrays, widths)], axis=along
    )
    result = lax.all_to_all(both, axis, split_axis=split_dim, concat_axis=concat_dim, tiled=True)
    parts = jnp.split(result, [sum(widths[:k]) for k in range(1, len(widths))], axis=along)
    return tuple(
        (b.reshape(*result.shape[:along], *a.shape[along:]) for a, b in zip(arrays, parts))
    )


def cut_along(x, dim, count):
    shape = x.shape
    parts = x.reshape(*shape[:dim], count, shape[dim] // count, *shape[dim + 1 :])
    return jnp.moveaxis(parts, dim, 0)


def in_order(parts, dim):
    parts = jnp.moveaxis(parts, 0, dim)
    shape = parts.shape
    return parts.reshape(*shape[:dim], shape[dim] * shape[dim + 1], *shape[dim + 2 :])


def exchange_in_order(parts, axes, turns):
    inside = parts.shape[1:]
    result = parts.reshape(*(lax.axis_size(a) for a in axes), *inside)
    for k in turns:
        result = lax.all_to_all(result, axes[k], k, k, tiled=True)
    return result.reshape(-1, *inside)


def core_and_chips(x, groups, turns, split_dim, concat_dim):
    count = lax.axis_size(groups[0]) * lax.axis_size(groups[1])
    parts = cut_along(x, split_dim, count)
    return in_order(exchange_in_order(parts, groups, turns), concat_dim)


def short_block(row_piece, others, weight):
    separation = row_piece[:, :, None] - others[:, None, :]
    nearness = (
        jnp.maximum(1.0 - jnp.sum(separation * separation, axis=0) / short_reach, 0.0)
        * weight[None, :]
    )
    return short_scale * jnp.sum(separation * nearness[None], axis=2)


def short_force(own, others, weight):
    row_count = own.shape[1]
    block_rows = min(512, row_count)
    pieces = own.reshape(3, row_count // block_rows, block_rows).transpose(1, 0, 2)
    result = lax.map(lambda row_piece: short_block(row_piece, others, weight), pieces)
    return result.transpose(1, 0, 2).reshape(3, row_count)


def tile_force(packet):
    separation = packet[0:3, :, None] - packet[4:7, None, :]
    nearness = (
        jnp.maximum(1.0 - jnp.sum(separation * separation, axis=0) / long_reach, 0.0)
        * packet[7][None, :]
    )
    return long_scale * packet[3][None, :] * jnp.sum(separation * nearness[None], axis=2)


def used_forces(packets, flags):

    def one_slot(item):
        return lax.cond(
            item[1] > 0.5, tile_force, lambda packet: jnp.zeros((3, 128), jnp.float32), item[0]
        )

    return lax.map(one_slot, (packets, flags))


def bonded_force(current, bonds, bond_k):
    bond_pull = bond_k[None, :] * (current[:, bonds[0]] - current[:, bonds[1]])
    zero_force = jnp.zeros_like(current)
    return zero_force.at[:, bonds[0]].add(-bond_pull).at[:, bonds[1]].add(bond_pull)


def neighbour_rows(stacked, halo_index):
    faces = jnp.moveaxis(stacked[:, halo_index], 1, 0)
    padded_x = padded(faces[0:2], (("gx", 0),), 1)
    padded_y = padded(faces[2:4], (("gy", 0),), 1)
    padded_z = padded(faces[4:6], ((GZ, 0),), 1)
    others = jnp.concatenate(
        [stacked, padded_x[0], padded_x[3], padded_y[0], padded_y[3], padded_z[0], padded_z[3]],
        axis=1,
    )
    unit = jnp.ones((halo_index.shape[1],), jnp.float32)
    lower_x = (lax.axis_index("gx") > 0).astype(jnp.float32)
    upper_x = (lax.axis_index("gx") < lax.axis_size("gx") - 1).astype(jnp.float32)
    lower_y = (lax.axis_index("gy") > 0).astype(jnp.float32)
    upper_y = (lax.axis_index("gy") < lax.axis_size("gy") - 1).astype(jnp.float32)
    lower_z = (lax.axis_index(GZ) > 0).astype(jnp.float32)
    upper_z = (lax.axis_index(GZ) < lax.axis_size(GZ) - 1).astype(jnp.float32)
    weight = jnp.concatenate(
        [
            jnp.ones((stacked.shape[1],), jnp.float32),
            unit * lower_x,
            unit * upper_x,
            unit * lower_y,
            unit * upper_y,
            unit * lower_z,
            unit * upper_z,
        ]
    )
    return (others, weight)


def on_device(
    positions,
    velocities,
    inv_mass,
    charge,
    fast_force,
    slow_force,
    bonds,
    bond_k,
    halo_index,
    pair_own,
    pair_partner,
    pair_count,
):
    half_inner = 0.5 * step_inner
    half_outer = 0.5 * INNER * step_inner
    moving = velocities + half_outer * inv_mass[None, :] * slow_force
    current = positions
    force_now = fast_force
    for inner_turn in range(INNER):
        moving = moving + half_inner * inv_mass[None, :] * force_now
        current = current + step_inner * moving
        stacked = jnp.concatenate([current, charge[None, :]], axis=0)
        others, weight = neighbour_rows(stacked, halo_index)
        force_now = short_force(current, others[:3], weight) + bonded_force(current, bonds, bond_k)
        moving = moving + half_inner * inv_mass[None, :] * force_now
    atom_count = current.shape[1]
    tile_count = atom_count // 128
    own_tiles = stacked.reshape(4, tile_count, 128).transpose(1, 0, 2)
    partners = others.reshape(4, others.shape[1] // 128, 128).transpose(1, 0, 2)
    slot_count = pair_own.shape[0]
    live_slots = (jnp.arange(slot_count) < pair_count[0]).astype(jnp.float32)
    own_rows = own_tiles[pair_own]
    packets = jnp.concatenate(
        [own_rows[:, :3], own_rows[:, 3:] * live_slots[:, None, None], partners[pair_partner]],
        axis=1,
    )
    groups = lax.axis_size("gy") * lax.axis_size(GZ)
    depth = slot_count // groups
    dealt = packets.reshape(depth, groups, 8, 128).transpose(1, 0, 2, 3)
    dealt_flags = live_slots.reshape(depth, groups).transpose(1, 0)
    arrived, arrived_flags = sent_together((dealt, dealt_flags), GY_GZ, 0, 0, 2)
    computed = used_forces(
        arrived.reshape(slot_count, 8, 128), arrived_flags.reshape(slot_count)
    ).reshape(groups, depth, 3, 128)
    returned = core_and_chips(computed, (("gy", "gz_0"), "gz_1"), (1, 0), 0, 0)
    tile_terms = returned.transpose(1, 0, 2, 3).reshape(slot_count, 3, 128)
    select = (pair_own[:, None] == jnp.arange(tile_count)[None, :]).astype(jnp.float32)
    slow_now = jnp.einsum(
        "st,sck->ctk", select, tile_terms, precision=lax.Precision.HIGHEST
    ).reshape(3, atom_count)
    moving = moving + half_outer * inv_mass[None, :] * slow_now
    return (current - positions, moving, force_now, slow_now)


def solution(mesh):
    torus = Mesh(
        mesh.devices.reshape(mesh.shape["gx"], mesh.shape["gy"], 4, 2), ("gx", "gy", "gz_0", "gz_1")
    )
    in_specs = (
        P(None, GX_GY_GZ),
        P(None, GX_GY_GZ),
        P(GX_GY_GZ),
        P(GX_GY_GZ),
        P(None, GX_GY_GZ),
        P(None, GX_GY_GZ),
        P(None, GX_GY_GZ),
        P(GX_GY_GZ),
        P(None, GX_GY_GZ),
        P(GX_GY_GZ),
        P(GX_GY_GZ),
        P(GX_GY_GZ),
    )
    out_specs = (P(None, GX_GY_GZ), P(None, GX_GY_GZ), P(None, GX_GY_GZ), P(None, GX_GY_GZ))
    return jax.shard_map(
        on_device, mesh=torus, in_specs=in_specs, out_specs=out_specs, check_vma=False
    )
```

profile of v0, /device:TPU:3, one launch (start us, length us, event | category | flops | bytes accessed | tf_op | source)
XLA Modules:
  0.0 594.9 jit_solution(1941221358676032089)
XLA Ops:
  21.9 6.3 %collective-permute-start.4 = (f32[1,4,256]{2,1,0:T(4,128)S(1)}, f32[1,4,256]{2,1,0:T(4,128)S(1)}, u32[]{:S(2)}, u32[]{:S(2)}) collective-permute-start(f32[1,4,256]{2,1,0:T(4,128)S(1)} %get-tuple-element.293), channel_id=1, source_target_pairs={{0,1},{1,2},{2,3},{3,4},{4,5},{5,6},{6,7},{8,9},{9,10},{10,11},{11... | collective-permute-start | bytes 12296 | tf_op jit(solution)/shard_map/ppermute | solution.py:27
  33.6 4.0 gather_fusion.1
  43.4 8.6 %while.50 = (s32[]{:T(128)}, f32[2,3,512]{2,1,0:T(4,128)S(1)}, f32[2,3,512]{2,1,0:T(4,128)S(1)}, f32[3,2560]{1,0:T(4,128)S(1)}, f32[2560]{0:T(1024)S(1)}, /*index=5*/s32[]{:T(128)}) while((s32[]{:T(128)}, f32[2,3,512]{2,1,0:T(4,128)S(1)}, f32[2,3,512]{2,1,0:T(4,128)S(1)}, f32[3,2560]{1,0:T(4,128)S(1)}, f32[2560]{0:T(1024)S(1)}, ...), condition=%wide.region_3.4_spmd, body=%wide.region_0.3_spmd.sunk | while | flops 27523584 | bytes 21090380 | solution.py:86
  52.2 6.2 %scatter_custom_fusion = f32[3,1024]{0,1:T(8,128)S(1)} fusion(f32[3,1024]{0,1:T(8,128)S(1)} %bitcast.172, s32[1024]{0:T(1024)S(1)} %bitcast.207, f32[1024,3]{1,0:T(8,128)S(1)} %copy-done.4, f32[1024,3]{1,0:T(8,128)S(1)} %gather_fusion.2, f32[1024]{0:T(1024)S(1)} %copy-done.6), kind=kCustom, calls=%fused_computation.78 | custom fusion | flops 12288 | bytes 1064960 | tf_op jit(solution)/shard_map/scatter-add | solution.py:112
  58.5 6.7 %scatter_custom_fusion.1 = f32[3,1024]{0,1:T(8,128)S(1)} fusion(f32[3,1024]{0,1:T(8,128)S(1)} %scatter_custom_fusion, s32[1024]{0:T(1024)S(1)} %bitcast.202, f32[1024,3]{1,0:T(8,128)S(1)} %copy-done.4, f32[1024,3]{1,0:T(8,128)S(1)} %gather_fusion.2, f32[1024]{0:T(1024)S(1)} %copy-done.6), kind=kCustom, calls=%fused_computation.94 | custom fusion | flops 9216 | bytes 1064960 | tf_op jit(solution)/shard_map/scatter-add | solution.py:112
  74.2 4.0 gather_fusion.4
  81.7 4.3 collective-permute-start.8
  87.3 4.1 collective-permute-start.10
  93.6 4.8 collective-permute-done.11
  98.4 8.5 %while.51 = (s32[]{:T(128)}, f32[2,3,512]{2,1,0:T(4,128)S(1)}, f32[2,3,512]{2,1,0:T(4,128)S(1)}, f32[3,2560]{1,0:T(4,128)S(1)}, f32[2560]{0:T(1024)S(1)}, /*index=5*/s32[]{:T(128)}) while((s32[]{:T(128)}, f32[2,3,512]{2,1,0:T(4,128)S(1)}, f32[2,3,512]{2,1,0:T(4,128)S(1)}, f32[3,2560]{1,0:T(4,128)S(1)}, f32[2560]{0:T(1024)S(1)}, ...), condition=%wide.region_9.10_spmd, body=%wide.region_6.9_spmd.sunk | while | flops 27523584 | bytes 21090380 | solution.py:86
  108.0 8.8 %scatter_custom_fusion.2 = f32[3,1024]{0,1:T(8,128)} fusion(f32[3,1024]{0,1:T(8,128)} %bitcast.42, s32[1024]{0:T(1024)S(1)} %bitcast.208, f32[1024,3]{1,0:T(8,128)} %gather_fusion.4, f32[1024,3]{1,0:T(8,128)S(1)} %gather_fusion.5, f32[1024]{0:T(1024)S(1)} %copy-done.6), kind=kCustom, calls=%fused_computation.76 | custom fusion | flops 12288 | bytes 1064960 | tf_op jit(solution)/shard_map/scatter-add | solution.py:112
  116.8 8.8 %scatter_custom_fusion.3 = f32[3,1024]{0,1:T(8,128)} fusion(f32[3,1024]{0,1:T(8,128)} %scatter_custom_fusion.2, s32[1024]{0:T(1024)S(1)} %bitcast.203, f32[1024,3]{1,0:T(8,128)} %gather_fusion.4, f32[1024,3]{1,0:T(8,128)S(1)} %gather_fusion.5, f32[1024]{0:T(1024)S(1)} %copy-done.6), kind=kCustom, calls=%fused_computation.95 | custom fusion | flops 9216 | bytes 1064960 | tf_op jit(solution)/shard_map/scatter-add | solution.py:112
  134.5 4.0 gather_fusion.8
  138.5 4.0 gather_fusion.7
  142.4 4.2 collective-permute-start.13
  146.7 4.0 collective-permute-start.14
  157.7 4.8 collective-permute-done.17
  162.5 8.6 %while.52 = (s32[]{:T(128)}, f32[2,3,512]{2,1,0:T(4,128)S(1)}, f32[2,3,512]{2,1,0:T(4,128)S(1)}, f32[3,2560]{1,0:T(4,128)S(1)}, f32[2560]{0:T(1024)S(1)}, /*index=5*/s32[]{:T(128)}) while((s32[]{:T(128)}, f32[2,3,512]{2,1,0:T(4,128)S(1)}, f32[2,3,512]{2,1,0:T(4,128)S(1)}, f32[3,2560]{1,0:T(4,128)S(1)}, f32[2560]{0:T(1024)S(1)}, ...), condition=%wide.region_15.16_spmd, body=%wide.region_12.15_spmd.sunk | while | flops 27523584 | bytes 21090380 | solution.py:86
  171.3 6.6 %scatter_custom_fusion.4 = f32[3,1024]{0,1:T(8,128)S(1)} fusion(f32[3,1024]{0,1:T(8,128)S(1)} %bitcast.171, s32[1024]{0:T(1024)S(1)} %bitcast.209, f32[1024,3]{1,0:T(8,128)} %gather_fusion.7, f32[1024,3]{1,0:T(8,128)S(1)} %copy-done.3, f32[1024]{0:T(1024)S(1)} %copy-done.6), kind=kCustom, calls=%fused_computation.74 | custom fusion | flops 12288 | bytes 552960 | tf_op jit(solution)/shard_map/scatter-add | solution.py:112
  178.0 6.6 %scatter_custom_fusion.5 = f32[3,1024]{0,1:T(8,128)S(1)} fusion(f32[3,1024]{0,1:T(8,128)S(1)} %scatter_custom_fusion.4, s32[1024]{0:T(1024)S(1)} %bitcast.204, f32[1024,3]{1,0:T(8,128)} %gather_fusion.7, f32[1024,3]{1,0:T(8,128)S(1)} %copy-done.3, f32[1024]{0:T(1024)S(1)} %copy-done.6), kind=kCustom, calls=%fused_computation.96 | custom fusion | flops 9216 | bytes 552960 | tf_op jit(solution)/shard_map/scatter-add | solution.py:112
  192.2 4.2 collective-permute-start.19
  196.5 4.0 collective-permute-start.20
  207.3 4.6 collective-permute-done.23
  217.0 9.9 %all-to-all-start = ((f32[32,6,1025]{2,1,0:T(8,128)}), f32[32,6,1025]{2,1,0:T(8,128)S(1)}, u32[]{:S(2)}, u32[]{:S(2)}) async-start(f32[32,6,1025]{2,1,0:T(8,128)} %copy.179), calls=%async_computation | async-start | bytes 2359296 | tf_op jit(solution)/shard_map/all_to_all | solution.py:40
  226.8 4.0 gather_fusion.11
  230.8 4.0 gather_fusion.10
  237.5 21.6 %all-to-all-done = f32[32,6,1025]{2,1,0:T(8,128)S(1)} async-done(((f32[32,6,1025]{2,1,0:T(8,128)}), f32[32,6,1025]{2,1,0:T(8,128)S(1)}, u32[]{:S(2)}, u32[]{:S(2)}) %all-to-all-start) | async-done | bytes 787232 | tf_op jit(solution)/shard_map/all_to_all | solution.py:40
  261.8 298.9 %while.54 = (s32[]{:T(128)}, f32[192,3,128]{2,1,0:T(4,128)S(1)}, f32[192]{0:T(256)S(1)}, f32[192,8,128]{2,1,0:T(8,128)S(1)}, s32[]{:T(128)}, /*index=5*/f32[1]{0:T(128)}) while((s32[]{:T(128)}, f32[192,3,128]{2,1,0:T(4,128)S(1)}, f32[192]{0:T(256)S(1)}, f32[192,8,128]{2,1,0:T(8,128)S(1)}, s32[]{:T(128)}, /*index=5*/f32[1]{0:T(128)}) %tuple.140), condition=%wide.region_29.30_spmd, body=%wide.region_24.29_spmd.sunk | while | flops 344196 | bytes 294527 | solution.py:106
  560.8 4.9 all_to_all.15
  570.2 8.6 %while.53 = (s32[]{:T(128)}, f32[2,3,512]{2,1,0:T(4,128)S(1)}, f32[2,3,512]{2,1,0:T(4,128)S(1)}, f32[3,2560]{1,0:T(4,128)S(1)}, f32[2560]{0:T(1024)S(1)}, /*index=5*/s32[]{:T(128)}) while((s32[]{:T(128)}, f32[2,3,512]{2,1,0:T(4,128)S(1)}, f32[2,3,512]{2,1,0:T(4,128)S(1)}, f32[3,2560]{1,0:T(4,128)S(1)}, f32[2560]{0:T(1024)S(1)}, ...), condition=%wide.region_21.22_spmd, body=%wide.region_18.21_spmd.sunk | while | flops 27523584 | bytes 21090380 | solution.py:86
  579.0 6.3 %scatter_custom_fusion.6 = f32[3,1024]{0,1:T(8,128)S(1)} fusion(f32[3,1024]{0,1:T(8,128)S(1)} %bitcast.170, s32[1024]{0:T(1024)} %bitcast.210, f32[1024,3]{1,0:T(8,128)S(1)} %copy-done.2, f32[1024,3]{1,0:T(8,128)S(1)} %copy-done.1, f32[1024]{0:T(1024)S(1)} %copy-done.6), kind=kCustom, calls=%fused_computation.72 | custom fusion | flops 12288 | bytes 1064960 | tf_op jit(solution)/shard_map/scatter-add | solution.py:112
  585.4 6.6 %scatter_custom_fusion.7 = f32[3,1024]{0,1:T(8,128)S(1)} fusion(f32[3,1024]{0,1:T(8,128)S(1)} %scatter_custom_fusion.6, s32[1024]{0:T(1024)} %bitcast.205, f32[1024,3]{1,0:T(8,128)S(1)} %copy-done.2, f32[1024,3]{1,0:T(8,128)S(1)} %copy-done.1, f32[1024]{0:T(1024)S(1)} %copy-done.6), kind=kCustom, calls=%fused_computation.97 | custom fusion | flops 9216 | bytes 1064960 | tf_op jit(solution)/shard_map/scatter-add | solution.py:112
  (1726 shorter events, 345.4 us)
Async XLA Ops:
  1.4 183.2 %copy-start.8 = (f32[1024]{0:T(1024)}, f32[1024]{0:T(1024)S(1)}, u32[]{:S(2)}) copy-start(f32[1024]{0:T(1024)S(1)} %get-tuple-element.301) | copy-start | bytes 12292
  11.2 26.4 %collective-permute-start = (f32[1,4,256]{2,1,0:T(4,128)S(1)}, f32[1,4,256]{2,1,0:T(4,128)S(1)}, u32[]{:S(2)}, u32[]{:S(2)}) collective-permute-start(f32[1,4,256]{2,1,0:T(4,128)S(1)} %get-tuple-element.297), channel_id=1, source_target_pairs={{0,32},{32,64},{64,96},{96,128},{128,160},{160,192},{192,224},{1,3... | collective-permute-start | bytes 12296 | tf_op jit(solution)/shard_map/ppermute | solution.py:27
  14.8 24.8 %collective-permute-start.1 = (f32[1,4,256]{2,1,0:T(4,128)S(1)}, f32[1,4,256]{2,1,0:T(4,128)S(1)}, u32[]{:S(2)}, u32[]{:S(2)}) collective-permute-start(f32[1,4,256]{2,1,0:T(4,128)S(1)} %get-tuple-element.296), channel_id=1, source_target_pairs={{32,0},{64,32},{96,64},{128,96},{160,128},{192,160},{224,192},{33,... | collective-permute-start | bytes 12296 | tf_op jit(solution)/shard_map/ppermute | solution.py:30
  17.4 22.1 %collective-permute-start.2 = (f32[1,4,256]{2,1,0:T(4,128)S(1)}, f32[1,4,256]{2,1,0:T(4,128)S(1)}, u32[]{:S(2)}, u32[]{:S(2)}) collective-permute-start(f32[1,4,256]{2,1,0:T(4,128)S(1)} %get-tuple-element.295), channel_id=1, source_target_pairs={{0,8},{8,16},{16,24},{1,9},{9,17},{17,25},{2,10},{10,18},{18,26},{... | collective-permute-start | bytes 12296 | tf_op jit(solution)/shard_map/ppermute | solution.py:27
  20.6 19.0 %collective-permute-start.3 = (f32[1,4,256]{2,1,0:T(4,128)S(1)}, f32[1,4,256]{2,1,0:T(4,128)S(1)}, u32[]{:S(2)}, u32[]{:S(2)}) collective-permute-start(f32[1,4,256]{2,1,0:T(4,128)S(1)} %get-tuple-element.294), channel_id=1, source_target_pairs={{8,0},{16,8},{24,16},{9,1},{17,9},{25,17},{10,2},{18,10},{26,18},{... | collective-permute-start | bytes 12296 | tf_op jit(solution)/shard_map/ppermute | solution.py:30
  21.9 17.7 %collective-permute-start.4 = (f32[1,4,256]{2,1,0:T(4,128)S(1)}, f32[1,4,256]{2,1,0:T(4,128)S(1)}, u32[]{:S(2)}, u32[]{:S(2)}) collective-permute-start(f32[1,4,256]{2,1,0:T(4,128)S(1)} %get-tuple-element.293), channel_id=1, source_target_pairs={{0,1},{1,2},{2,3},{3,4},{4,5},{5,6},{6,7},{8,9},{9,10},{10,11},{11... | collective-permute-start | bytes 12296 | tf_op jit(solution)/shard_map/ppermute | solution.py:27
  28.5 142.8 %copy-start.19 = (s32[1024,1]{0,1:T(1,128)}, s32[1024,1]{0,1:T(1,128)S(1)}, u32[]{:S(2)}) copy-start(s32[1024,1]{0,1:T(1,128)S(1)} %get-tuple-element.299) | copy-start | bytes 12292
  28.5 149.4 %copy-start.18 = (s32[1024,1]{0,1:T(1,128)}, s32[1024,1]{0,1:T(1,128)S(1)}, u32[]{:S(2)}) copy-start(s32[1024,1]{0,1:T(1,128)S(1)} %get-tuple-element.298) | copy-start | bytes 12292
  28.6 109.9 %copy-start.10 = (s32[1024]{0:T(1024)}, s32[1024]{0:T(1024)S(1)}, u32[]{:S(2)}) copy-start(s32[1024]{0:T(1024)S(1)} %broadcast_clamp_fusion.1) | copy-start | bytes 12292
  30.5 103.9 %copy-start.12 = (s32[1024]{0:T(1024)}, s32[1024]{0:T(1024)S(1)}, u32[]{:S(2)}) copy-start(s32[1024]{0:T(1024)S(1)} %get-tuple-element.305) | copy-start | bytes 12292
  37.6 5.8 collective-permute-start.5
  68.7 22.9 %collective-permute-start.6 = (f32[1,4,256]{2,1,0:T(4,128)S(1)}, f32[1,4,256]{2,1,0:T(4,128)S(1)}, u32[]{:S(2)}, u32[]{:S(2)}) collective-permute-start(f32[1,4,256]{2,1,0:T(4,128)S(1)} %get-tuple-element.291), channel_id=1, source_target_pairs={{0,32},{32,64},{64,96},{96,128},{128,160},{160,192},{192,224},{1,3... | collective-permute-start | bytes 12296 | tf_op jit(solution)/shard_map/ppermute | solution.py:27
  78.2 15.3 %collective-permute-start.7 = (f32[1,4,256]{2,1,0:T(4,128)S(1)}, f32[1,4,256]{2,1,0:T(4,128)S(1)}, u32[]{:S(2)}, u32[]{:S(2)}) collective-permute-start(f32[1,4,256]{2,1,0:T(4,128)S(1)} %get-tuple-element.290), channel_id=1, source_target_pairs={{32,0},{64,32},{96,64},{128,96},{160,128},{192,160},{224,192},{33,... | collective-permute-start | bytes 12296 | tf_op jit(solution)/shard_map/ppermute | solution.py:30
  81.7 11.8 %collective-permute-start.8 = (f32[1,4,256]{2,1,0:T(4,128)S(1)}, f32[1,4,256]{2,1,0:T(4,128)S(1)}, u32[]{:S(2)}, u32[]{:S(2)}) collective-permute-start(f32[1,4,256]{2,1,0:T(4,128)S(1)} %get-tuple-element.289), channel_id=1, source_target_pairs={{0,8},{8,16},{16,24},{1,9},{9,17},{17,25},{2,10},{10,18},{18,26},{... | collective-permute-start | bytes 12296 | tf_op jit(solution)/shard_map/ppermute | solution.py:27
  86.0 7.6 %collective-permute-start.9 = (f32[1,4,256]{2,1,0:T(4,128)S(1)}, f32[1,4,256]{2,1,0:T(4,128)S(1)}, u32[]{:S(2)}, u32[]{:S(2)}) collective-permute-start(f32[1,4,256]{2,1,0:T(4,128)S(1)} %get-tuple-element.288), channel_id=1, source_target_pairs={{8,0},{16,8},{24,16},{9,1},{17,9},{25,17},{10,2},{18,10},{26,18},{... | collective-permute-start | bytes 12296 | tf_op jit(solution)/shard_map/ppermute | solution.py:30
  87.3 6.3 %collective-permute-start.10 = (f32[1,4,256]{2,1,0:T(4,128)S(1)}, f32[1,4,256]{2,1,0:T(4,128)S(1)}, u32[]{:S(2)}, u32[]{:S(2)}) collective-permute-start(f32[1,4,256]{2,1,0:T(4,128)S(1)} %get-tuple-element.287), channel_id=1, source_target_pairs={{0,1},{1,2},{2,3},{3,4},{4,5},{5,6},{6,7},{8,9},{9,10},{10,11},{11... | collective-permute-start | bytes 12296 | tf_op jit(solution)/shard_map/ppermute | solution.py:27
  91.5 6.8 %collective-permute-start.11 = (f32[1,4,256]{2,1,0:T(4,128)S(1)}, f32[1,4,256]{2,1,0:T(4,128)S(1)}, u32[]{:S(2)}, u32[]{:S(2)}) collective-permute-start(f32[1,4,256]{2,1,0:T(4,128)S(1)} %get-tuple-element.286), channel_id=1, source_target_pairs={{1,0},{2,1},{3,2},{4,3},{5,4},{6,5},{7,6},{9,8},{10,9},{11,10},{12... | collective-permute-start | bytes 12296 | tf_op jit(solution)/shard_map/ppermute | solution.py:30
  132.5 23.0 %collective-permute-start.12 = (f32[1,4,256]{2,1,0:T(4,128)S(1)}, f32[1,4,256]{2,1,0:T(4,128)S(1)}, u32[]{:S(2)}, u32[]{:S(2)}) collective-permute-start(f32[1,4,256]{2,1,0:T(4,128)S(1)} %get-tuple-element.285), channel_id=1, source_target_pairs={{0,32},{32,64},{64,96},{96,128},{128,160},{160,192},{192,224},{1,3... | collective-permute-start | bytes 12296 | tf_op jit(solution)/shard_map/ppermute | solution.py:27
  142.4 15.1 %collective-permute-start.13 = (f32[1,4,256]{2,1,0:T(4,128)S(1)}, f32[1,4,256]{2,1,0:T(4,128)S(1)}, u32[]{:S(2)}, u32[]{:S(2)}) collective-permute-start(f32[1,4,256]{2,1,0:T(4,128)S(1)} %get-tuple-element.284), channel_id=1, source_target_pairs={{32,0},{64,32},{96,64},{128,96},{160,128},{192,160},{224,192},{33,... | collective-permute-start | bytes 12296 | tf_op jit(solution)/shard_map/ppermute | solution.py:30
  146.7 10.9 %collective-permute-start.14 = (f32[1,4,256]{2,1,0:T(4,128)S(1)}, f32[1,4,256]{2,1,0:T(4,128)S(1)}, u32[]{:S(2)}, u32[]{:S(2)}) collective-permute-start(f32[1,4,256]{2,1,0:T(4,128)S(1)} %get-tuple-element.283), channel_id=1, source_target_pairs={{0,8},{8,16},{16,24},{1,9},{9,17},{17,25},{2,10},{10,18},{18,26},{... | collective-permute-start | bytes 12296 | tf_op jit(solution)/shard_map/ppermute | solution.py:27
  150.7 6.9 %collective-permute-start.15 = (f32[1,4,256]{2,1,0:T(4,128)S(1)}, f32[1,4,256]{2,1,0:T(4,128)S(1)}, u32[]{:S(2)}, u32[]{:S(2)}) collective-permute-start(f32[1,4,256]{2,1,0:T(4,128)S(1)} %get-tuple-element.282), channel_id=1, source_target_pairs={{8,0},{16,8},{24,16},{9,1},{17,9},{25,17},{10,2},{18,10},{26,18},{... | collective-permute-start | bytes 12296 | tf_op jit(solution)/shard_map/ppermute | solution.py:30
  152.0 5.7 collective-permute-start.16
  155.5 7.0 %collective-permute-start.17 = (f32[1,4,256]{2,1,0:T(4,128)S(1)}, f32[1,4,256]{2,1,0:T(4,128)S(1)}, u32[]{:S(2)}, u32[]{:S(2)}) collective-permute-start(f32[1,4,256]{2,1,0:T(4,128)S(1)} %get-tuple-element.280), channel_id=1, source_target_pairs={{1,0},{2,1},{3,2},{4,3},{5,4},{6,5},{7,6},{9,8},{10,9},{11,10},{12... | collective-permute-start | bytes 12296 | tf_op jit(solution)/shard_map/ppermute | solution.py:30
  188.9 16.2 %collective-permute-start.18 = (f32[1,4,256]{2,1,0:T(4,128)S(1)}, f32[1,4,256]{2,1,0:T(4,128)S(1)}, u32[]{:S(2)}, u32[]{:S(2)}) collective-permute-start(f32[1,4,256]{2,1,0:T(4,128)S(1)} %get-tuple-element.279), channel_id=1, source_target_pairs={{0,32},{32,64},{64,96},{96,128},{128,160},{160,192},{192,224},{1,3... | collective-permute-start | bytes 12296 | tf_op jit(solution)/shard_map/ppermute | solution.py:27
  192.2 15.0 %collective-permute-start.19 = (f32[1,4,256]{2,1,0:T(4,128)S(1)}, f32[1,4,256]{2,1,0:T(4,128)S(1)}, u32[]{:S(2)}, u32[]{:S(2)}) collective-permute-start(f32[1,4,256]{2,1,0:T(4,128)S(1)} %get-tuple-element.278), channel_id=1, source_target_pairs={{32,0},{64,32},{96,64},{128,96},{160,128},{192,160},{224,192},{33,... | collective-permute-start | bytes 12296 | tf_op jit(solution)/shard_map/ppermute | solution.py:30
  196.5 10.8 %collective-permute-start.20 = (f32[1,4,256]{2,1,0:T(4,128)S(1)}, f32[1,4,256]{2,1,0:T(4,128)S(1)}, u32[]{:S(2)}, u32[]{:S(2)}) collective-permute-start(f32[1,4,256]{2,1,0:T(4,128)S(1)} %get-tuple-element.277), channel_id=1, source_target_pairs={{0,8},{8,16},{16,24},{1,9},{9,17},{17,25},{2,10},{10,18},{18,26},{... | collective-permute-start | bytes 12296 | tf_op jit(solution)/shard_map/ppermute | solution.py:27
  200.5 6.8 %collective-permute-start.21 = (f32[1,4,256]{2,1,0:T(4,128)S(1)}, f32[1,4,256]{2,1,0:T(4,128)S(1)}, u32[]{:S(2)}, u32[]{:S(2)}) collective-permute-start(f32[1,4,256]{2,1,0:T(4,128)S(1)} %get-tuple-element.276), channel_id=1, source_target_pairs={{8,0},{16,8},{24,16},{9,1},{17,9},{25,17},{10,2},{18,10},{26,18},{... | collective-permute-start | bytes 12296 | tf_op jit(solution)/shard_map/ppermute | solution.py:30
  201.8 5.5 collective-permute-start.22
  205.1 6.8 %collective-permute-start.23 = (f32[1,4,256]{2,1,0:T(4,128)S(1)}, f32[1,4,256]{2,1,0:T(4,128)S(1)}, u32[]{:S(2)}, u32[]{:S(2)}) collective-permute-start(f32[1,4,256]{2,1,0:T(4,128)S(1)} %get-tuple-element.274), channel_id=1, source_target_pairs={{1,0},{2,1},{3,2},{4,3},{5,4},{6,5},{7,6},{9,8},{10,9},{11,10},{12... | collective-permute-start | bytes 12296 | tf_op jit(solution)/shard_map/ppermute | solution.py:30
  217.0 42.1 %all-to-all-start = ((f32[32,6,1025]{2,1,0:T(8,128)}), f32[32,6,1025]{2,1,0:T(8,128)S(1)}, u32[]{:S(2)}, u32[]{:S(2)}) async-start(f32[32,6,1025]{2,1,0:T(8,128)} %copy.179), calls=%async_computation | async-start | bytes 2359296 | tf_op jit(solution)/shard_map/all_to_all | solution.py:40
  235.6 334.5 %copy-start.7 = (f32[3,2,512]{2,0,1:T(4,128)S(1)}, f32[3,2,512]{2,0,1:T(4,128)}, u32[]{:S(2)}) copy-start(f32[3,2,512]{2,0,1:T(4,128)} %copy.171) | copy-start | bytes 36868
  566.6 26.2 %all-to-all-start.2 = ((f32[16,2,1,6,3,128]{5,1,4,3,2,0:T(2,128)}), f32[16,2,1,6,3,128]{5,1,4,3,2,0:T(2,128)S(1)}, u32[]{:S(2)}, u32[]{:S(2)}) async-start(f32[16,2,1,6,3,128]{5,1,4,3,2,0:T(2,128)} %copy.182), calls=%async_computation.2 | async-start | bytes 589824 | tf_op jit(solution)/shard_map/all_to_all | solution.py:63
  (18 other events, 379.0 us)
where the time goes:
time: 607 us; the launch traced here: 595 us
  local copies, waits for them, and re-layouts  181 us (30%)
  other arithmetic  144 us (24%)
  loops' own time  138 us (23%)
  starting transfers between devices  83.7 us (14%)
  waiting for transfers between devices  39.6 us (7%)
    another operation x1, loops' own time, used_forces(): return lax.map(one_slot, (packets, flags))  130 us
    dynamic_slice x311, local copies, waits for them, and re-layouts, used_forces(): return lax.map(one_slot, (packets, flags))  114 us
    scatter-add x8, other arithmetic, bonded_force(): zero_force.at[:, bonds[0]].add(-bond_pull).at[:, bonds[1]].add(bond_pull)  56.6 us
    ppermute x12, starting transfers between devices, padded(): lax.ppermute(lax.slice_in_dim(block, block.shape[dim] - width, None, axis...  42.5 us
    gather x8, local copies, waits for them, and re-layouts, bonded_force(): bond_pull = bond_k[None, :] * (current[:, bonds[0]] - current[:, bonds[1]])  29.6 us
    ppermute x12, starting transfers between devices, padded(): lax.ppermute(lax.slice_in_dim(block, 0, width, axis=dim), axis, backward)  27.9 us
    reduce_sum x119, other arithmetic, tile_force(): jnp.sum(separation * nearness[None], axis=2)  26.9 us
    all_to_all x1, waiting for transfers between devices, sent_together(): lax.all_to_all(both, axis, split_axis=split_dim, concat_axis=concat_dim,...  21.6 us
  transfers between devices with their start and end apart: 26, of which 5 were waited for; matrix products, arithmetic and copies ran while one was open for 10% of the time, Pallas kernels for 0%

commit v1 on v0

v1 whole, which is shorter than its diff:
```python
import functools

import jax
import jax.numpy as jnp
from jax import lax
from jax.experimental import pallas as pl
from jax.experimental.pallas import tpu as pltpu
from jax.sharding import PartitionSpec as P

MESH = pl.DeviceIdType.MESH
F32 = jnp.float32
BF16 = jnp.bfloat16

INNER = 4
STEP = 0.1
SIDE = 4.0
SHORT_SCALE = 1.0
SHORT_INV = 1.0 / 0.64
LONG_SCALE = 0.5
LONG_INV = 1.0 / 1.44
FAR = 1e30

ATOMS = 1024
HALO = 256
FACES = 6
VISIBLE = ATOMS + FACES * HALO
BLOCK = 256
KDIM = 48
TILE = 128
OWN_TILES = ATOMS // TILE
SLOTS = 192
AXES = ("gx", "gy", "gz")


def rows_like(shape):
    return lax.broadcasted_iota(jnp.int32, shape, 0)


def lanes_like(shape):
    return lax.broadcasted_iota(jnp.int32, shape, 1)


def split3(a):
    high = a.astype(BF16).astype(F32)
    rest = a - high
    mid = rest.astype(BF16).astype(F32)
    return high, mid, rest - mid


def left_rows(a):
    high, mid, low = split3(a)
    return jnp.concatenate([high, high, high, mid, mid, low], axis=0)


def right_rows(a):
    high, mid, low = split3(a)
    return jnp.concatenate([high, mid, low, high, mid, high], axis=0)


def featured(x, q):
    row = rows_like(x.shape)
    square = jnp.sum(jnp.where(row < 3, x * x, 0.0), axis=0, keepdims=True)
    return jnp.where(
        row < 3, x, jnp.where(row == 3, square, jnp.where(row == 4, 1.0, jnp.where(row == 5, q, 0.0)))
    )


def partner_side(features, inverse):
    row = rows_like(features.shape)
    square = features[3:4, :]
    return jnp.where(
        row < 3,
        (2.0 * inverse) * features,
        jnp.where(row == 3, -inverse, jnp.where(row == 4, 1.0 - inverse * square, 0.0)),
    )


def pick_rows(features):
    count = len(features)
    shape = (KDIM, count * TILE)
    row, lane = rows_like(shape), lanes_like(shape)
    out = jnp.zeros(shape, F32)
    for block, f in enumerate(features):
        part = (row == f) | (row == 24 + f) | (row == 40 + f)
        out = jnp.where(part & (lane // TILE == block), 1.0, out)
    return out


def kernel(
    pos, vel, inv_mass, charge, fast, slow, bonds, bond_k, halo, own_slot, partner_slot, count,
    disp_out, vel_out, fast_out, slow_out,
    x_ref, v_ref, f_ref, start_ref, send, recv, left, right, near, incid, onehot, mult, total, slots,
    send_sem, recv_sem,
):
    place = [lax.axis_index(a) for a in AXES]
    extent = [lax.axis_size(a) for a in AXES]
    exists = []
    target = []
    for face in range(FACES):
        axis, high = face // 2, face % 2
        exists.append(place[axis] < extent[axis] - 1 if high else place[axis] > 0)
        target.append({AXES[axis]: place[axis] + 1 if high else place[axis] - 1})

    recv[...] = jnp.zeros_like(recv)

    barrier = pltpu.get_barrier_semaphore()
    for face in range(FACES):

        @pl.when(exists[face])
        def _(face=face):
            pl.semaphore_signal(barrier, inc=1, device_id=target[face], device_id_type=MESH)

    wide = (8, ATOMS)
    row = rows_like(wide)
    centre = jnp.where(
        row == 0, place[0].astype(F32), jnp.where(row == 1, place[1].astype(F32), place[2].astype(F32))
    ) * SIDE + 0.5 * SIDE
    x_ref[...] = jnp.zeros(wide, F32)
    v_ref[...] = jnp.zeros(wide, F32)
    f_ref[...] = jnp.zeros(wide, F32)
    x_ref[0:3, :] = pos[...] - centre[0:3, :]
    mass = inv_mass[...]
    v_ref[0:3, :] = vel[...] + (0.5 * INNER * STEP) * mass * slow[...]
    f_ref[0:3, :] = fast[...]
    start_ref[...] = x_ref[...]

    chunk = 128

    def build(c, _):
        base = pl.multiple_of(c * chunk, chunk)
        atom = rows_like((chunk, ATOMS)) + base
        first = jnp.where(atom == bonds[0:1, :], 1.0, 0.0)
        second = jnp.where(atom == bonds[1:2, :], 1.0, 0.0)
        incid[pl.ds(base, chunk), :] = (first - second).astype(BF16)
        atom = rows_like((chunk, HALO)) + base
        for face in range(FACES):
            hit = jnp.where(atom == halo[face : face + 1, :], 1.0, 0.0)
            onehot[pl.ds(base, chunk), face * HALO : (face + 1) * HALO] = hit.astype(BF16)
        return 0

    lax.fori_loop(0, ATOMS // chunk, build, 0)

    right[:, ATOMS : ATOMS + 4 * TILE] = pick_rows((0, 1, 2, 5)).astype(BF16)

    slots[...] = jnp.full(slots.shape, -1, jnp.int32)
    slots[0:1, 0:SLOTS] = own_slot[...]
    slots[1:2, 0:SLOTS] = partner_slot[...]
    slot_lane = lanes_like((ATOMS, 2 * TILE))
    tile_of = rows_like((ATOMS, 2 * TILE)) // TILE
    own_hit = jnp.where((tile_of == slots[0:1, :]) & (slot_lane < count[0, 0]), 1.0, 0.0).astype(BF16)
    partner_hit = jnp.where(rows_like((32, 2 * TILE)) == slots[1:2, :], 1.0, 0.0).astype(BF16)
    mult[...] = lax.dot_general(partner_hit, own_hit, (((1,), (1,)), ((), ())), preferred_element_type=F32)

    arrivals = exists[0].astype(jnp.int32)
    for face in range(1, FACES):
        arrivals = arrivals + exists[face].astype(jnp.int32)
    pl.semaphore_wait(barrier, arrivals)

    face_row = rows_like((8, HALO))

    def copy_out(k, face):
        return pltpu.make_async_remote_copy(
            src_ref=send.at[k, face],
            dst_ref=recv.at[k, face ^ 1],
            send_sem=send_sem.at[k, face],
            recv_sem=recv_sem.at[k, face ^ 1],
            device_id=target[face],
            device_id_type=MESH,
        )

    def short_blocks(first, last, acc):
        def one_block(b, acc):
            base = pl.multiple_of(b * BLOCK, BLOCK)
            near[:, 0 : ATOMS + 3 * TILE] = jnp.dot(
                left[pl.ds(base, BLOCK), :], right[:, 0 : ATOMS + 3 * TILE], preferred_element_type=F32
            )

            def group(g, acc):
                at = pl.ds(pl.multiple_of(g * 8, 8), 8)
                xj = [near[at, ATOMS + c * TILE : ATOMS + (c + 1) * TILE] for c in range(3)]
                out = []
                for t in range(OWN_TILES):
                    n = jnp.maximum(near[at, t * TILE : (t + 1) * TILE], 0.0)
                    s, fx, fy, fz = acc[4 * t : 4 * t + 4]
                    out += [s + n, fx + n * xj[0], fy + n * xj[1], fz + n * xj[2]]
                return tuple(out)

            return lax.fori_loop(0, BLOCK // 8, group, acc, unroll=8)

        return lax.fori_loop(first, last, one_block, acc)

    def gathered(acc, x):
        parts = []
        for t in range(OWN_TILES):
            s, fx, fy, fz = [jnp.sum(a, axis=0, keepdims=True) for a in acc[4 * t : 4 * t + 4]]
            r = rows_like((8, TILE))
            moved = jnp.where(r == 0, fx, jnp.where(r == 1, fy, jnp.where(r == 2, fz, 0.0)))
            parts.append(x[:, t * TILE : (t + 1) * TILE] * s - moved)
        return jnp.concatenate(parts, axis=1)

    zero_acc = tuple(jnp.zeros((8, TILE), F32) for _ in range(4 * OWN_TILES))

    def inner(k, _):
        v = v_ref[...] + (0.5 * STEP) * mass * f_ref[...]
        x = x_ref[...] + STEP * v
        v_ref[...] = v
        x_ref[...] = x
        features = featured(x, charge[...])
        rows = left_rows(features)
        high, mid, low = rows[0:8], rows[24:32], rows[40:48]
        parts = jnp.concatenate([high, mid, low], axis=0).astype(BF16)

        picked = jnp.dot(parts, onehot[...], preferred_element_type=F32)
        picked = picked[0:8] + picked[8:16] + picked[16:24]
        for face in range(FACES):
            send[k, face] = picked[:, face * HALO : (face + 1) * HALO]
        for face in range(FACES):

            @pl.when(exists[face])
            def _(face=face):
                copy_out(k, face).start()

        left[0:ATOMS, :] = rows.T.astype(BF16)
        right[:, 0:ATOMS] = right_rows(partner_side(features, SHORT_INV)).astype(BF16)

        apart = jnp.dot(parts, incid[...], preferred_element_type=F32)
        apart = apart[0:8] + apart[8:16] + apart[16:24]
        pull = split3(bond_k[...] * apart)
        pull = jnp.concatenate(pull, axis=0).astype(BF16)
        drawn = lax.dot_general(pull, incid[...], (((1,), (1,)), ((), ())), preferred_element_type=F32)
        f_ref[...] = -(drawn[0:8] + drawn[8:16] + drawn[16:24])

        acc = short_blocks(0, ATOMS // BLOCK, zero_acc)

        for face in range(FACES):

            @pl.when(exists[face])
            def _(face=face):
                copy_out(k, face ^ 1).wait_recv()

        for face in range(FACES):
            axis = face // 2
            shift = SIDE if face % 2 else -SIDE
            got = recv[k, face]
            seen = jnp.where(exists[face], jnp.ones((8, HALO), F32), 0.0) > 0.0
            moved = jnp.where(seen, got + jnp.where(face_row == axis, shift, 0.0), 0.0)
            there = featured(moved, moved[5:6, :])
            there = jnp.where(seen | (face_row != 3), there, FAR)
            base = ATOMS + face * HALO
            left[base : base + HALO, :] = left_rows(there).T.astype(BF16)

        acc = short_blocks(ATOMS // BLOCK, VISIBLE // BLOCK, acc)
        force = f_ref[...] + SHORT_SCALE * gathered(acc, x)
        force = jnp.where(row < 3, force, 0.0)
        f_ref[...] = force
        v_ref[...] = v_ref[...] + (0.5 * STEP) * mass * force

        for face in range(FACES):

            @pl.when(exists[face])
            def _(face=face):
                copy_out(k, face).wait_send()

        return 0

    lax.fori_loop(0, INNER, inner, 0)

    x = x_ref[...]
    features = featured(x, charge[...])
    right[:, 0:ATOMS] = right_rows(partner_side(features, LONG_INV)).astype(BF16)
    total[...] = jnp.zeros_like(total)

    def long_block(b, _):
        base = pl.multiple_of(b * TILE, TILE)
        near[0:TILE, :] = jnp.dot(left[pl.ds(base, TILE), :], right[...], preferred_element_type=F32)

        def group(g, acc):
            at = pl.ds(pl.multiple_of(g * 8, 8), 8)
            xj = [near[at, ATOMS + c * TILE : ATOMS + (c + 1) * TILE] for c in range(4)]
            out = []
            for t in range(OWN_TILES):
                n = jnp.maximum(near[at, t * TILE : (t + 1) * TILE], 0.0) * xj[3]
                s, fx, fy, fz = acc[4 * t : 4 * t + 4]
                out += [s + n, fx + n * xj[0], fy + n * xj[1], fz + n * xj[2]]
            return tuple(out)

        acc = lax.fori_loop(0, TILE // 8, group, zero_acc, unroll=8)
        times = mult[pl.ds(b, 1), :]
        for t in range(OWN_TILES):
            m = times[:, t * TILE : (t + 1) * TILE]
            for c in range(4):
                total[4 * t + c] = total[4 * t + c] + m * acc[4 * t + c]
        return 0

    lax.fori_loop(0, VISIBLE // TILE, long_block, 0)
    acc = [total[i] for i in range(4 * OWN_TILES)]
    slow_now = LONG_SCALE * charge[...] * gathered(acc, x)
    slow_out[...] = slow_now[0:3, :]
    fast_out[...] = f_ref[0:3, :]
    disp_out[...] = (x - start_ref[...])[0:3, :]
    vel_out[...] = v_ref[0:3, :] + (0.5 * INNER * STEP) * mass * slow_now[0:3, :]


def on_device(pos, vel, inv_mass, charge, fast, slow, bonds, bond_k, halo, own_slot, partner_slot, count):
    vmem = pl.BlockSpec(memory_space=pltpu.VMEM)
    smem = pl.BlockSpec(memory_space=pltpu.SMEM)
    out = jax.ShapeDtypeStruct((3, ATOMS), F32)
    return pl.pallas_call(
        kernel,
        out_shape=(out, out, out, out),
        in_specs=[vmem] * 11 + [smem],
        out_specs=(vmem,) * 4,
        scratch_shapes=[
            pltpu.VMEM((8, ATOMS), F32),
            pltpu.VMEM((8, ATOMS), F32),
            pltpu.VMEM((8, ATOMS), F32),
            pltpu.VMEM((8, ATOMS), F32),
            pltpu.VMEM((INNER, FACES, 8, HALO), F32),
            pltpu.VMEM((INNER, FACES, 8, HALO), F32),
            pltpu.VMEM((VISIBLE, KDIM), BF16),
            pltpu.VMEM((KDIM, ATOMS + 4 * TILE), BF16),
            pltpu.VMEM((BLOCK, ATOMS + 4 * TILE), F32),
            pltpu.VMEM((ATOMS, ATOMS), BF16),
            pltpu.VMEM((ATOMS, FACES * HALO), BF16),
            pltpu.VMEM((32, ATOMS), F32),
            pltpu.VMEM((4 * OWN_TILES, 8, TILE), F32),
            pltpu.VMEM((8, 2 * TILE), jnp.int32),
            pltpu.SemaphoreType.DMA((INNER, FACES)),
            pltpu.SemaphoreType.DMA((INNER, FACES)),
        ],
        compiler_params=pltpu.CompilerParams(collective_id=0, has_side_effects=True),
        name="outer_step",
    )(
        pos, vel, inv_mass[None, :], charge[None, :], fast, slow, bonds, bond_k[None, :], halo,
        own_slot[None, :], partner_slot[None, :], count[None, :],
    )


def solution(mesh):
    both = P(None, AXES)
    line = P(AXES)
    return jax.shard_map(
        on_device,
        mesh=mesh,
        in_specs=(both, both, line, line, both, both, both, line, both, line, line, line),
        out_specs=(both, both, both, both),
        check_vma=False,
    )
```

time: 607 us -> 53.9 us (0.09)
  the two profiles are of different devices: /device:TPU:3 before, /device:TPU:1 now
where the time goes in v1:
time: 53.9 us; the launch traced here: 53.1 us
  Pallas kernels  48.4 us (90%)
  local copies, waits for them, and re-layouts  3.39 us (6%)
  between operations  1.3 us (2%)
    pallas_call x1, Pallas kernels, on_device(): pl.pallas_call(kernel, out_shape=(out, out, out, out), in_specs=[vmem] *...  48.4 us
    unnamed x10, local copies, waits for them, and re-layouts  3.39 us

profile of v1, /device:TPU:1, one launch (start us, length us, event | category | flops | bytes accessed | tf_op | source)
XLA Modules:
  0.0 53.1 jit_solution(18028941549011032147)
XLA Ops:
  1.3 48.4 %outer_step.1 = (f32[3,1024]{1,0:T(4,128)}, f32[3,1024]{1,0:T(4,128)}, f32[3,1024]{1,0:T(4,128)}, f32[3,1024]{1,0:T(4,128)}) custom-call(f32[3,1024]{1,0:T(4,128)} %pos.1, f32[3,1024]{1,0:T(4,128)} %vel.1, f32[1,1024]{1,0:T(1,128)} %bitcast.7, f32[1,1024]{1,0:T(1,128)} %bitcast.8, f32[3,1024]{1,0:T(4,128)} %fast.1, f32[3,1024]{1,0:T(4,128)} %slow.1, ...), custom_call_target="tpu_custom_call" | custom-call | tf_op jit(solution)/shard_map/outer_step/pallas_call | solution.py:308
  49.7 0.0 copy-start.2
  49.7 1.3 %copy.21 = f32[3,1024]{1,0:T(4,128)} copy(f32[3,1024]{1,0:T(4,128)} %get-tuple-element.8) | data formatting | bytes 24576
  51.0 0.0 copy-done.2
  51.0 0.0 copy-start.1
  51.0 0.6 %copy.22 = f32[3,1024]{1,0:T(4,128)} copy(f32[3,1024]{1,0:T(4,128)S(1)} %copy-done.2) | data formatting | bytes 24576
  51.6 0.1 copy-done.1
  51.7 0.0 copy-start
  51.7 0.6 %copy.23 = f32[3,1024]{1,0:T(4,128)} copy(f32[3,1024]{1,0:T(4,128)S(1)} %copy-done.1) | data formatting | bytes 24576
  52.4 0.1 copy-done
  52.5 0.6 %copy.24 = f32[3,1024]{1,0:T(4,128)} copy(f32[3,1024]{1,0:T(4,128)S(1)} %copy-done) | data formatting | bytes 24576
Async XLA Ops:
  49.7 1.3 %copy-start.2 = (f32[3,1024]{1,0:T(4,128)S(1)}, f32[3,1024]{1,0:T(4,128)}, u32[]{:S(2)}) copy-start(f32[3,1024]{1,0:T(4,128)} %get-tuple-element.9) | copy-start | bytes 36868
  51.0 0.7 %copy-start.1 = (f32[3,1024]{1,0:T(4,128)S(1)}, f32[3,1024]{1,0:T(4,128)}, u32[]{:S(2)}) copy-start(f32[3,1024]{1,0:T(4,128)} %get-tuple-element.10) | copy-start | bytes 36868
  51.7 0.7 %copy-start = (f32[3,1024]{1,0:T(4,128)S(1)}, f32[3,1024]{1,0:T(4,128)}, u32[]{:S(2)}) copy-start(f32[3,1024]{1,0:T(4,128)} %get-tuple-element.11) | copy-start | bytes 36868

commit v2 on v1

--- a/solution.py
+++ b/solution.py
@@ -89,7 +89,7 @@
 def kernel(
     pos, vel, inv_mass, charge, fast, slow, bonds, bond_k, halo, own_slot, partner_slot, count,
     disp_out, vel_out, fast_out, slow_out,
-    x_ref, v_ref, f_ref, start_ref, send, recv, left, right, near, incid, onehot, mult, total, slots,
+    x_ref, v_ref, f_ref, start_ref, send, recv, left, right, spread, incid, mult, slots,
     send_sem, recv_sem,
 ):
     place = [lax.axis_index(a) for a in AXES]
@@ -124,18 +124,14 @@
     f_ref[0:3, :] = fast[...]
     start_ref[...] = x_ref[...]
 
+    stiff = jnp.where(bonds[0:1, :] == bonds[1:2, :], 0.0, bond_k[...])
     chunk = 128
 
     def build(c, _):
         base = pl.multiple_of(c * chunk, chunk)
         atom = rows_like((chunk, ATOMS)) + base
-        first = jnp.where(atom == bonds[0:1, :], 1.0, 0.0)
-        second = jnp.where(atom == bonds[1:2, :], 1.0, 0.0)
-        incid[pl.ds(base, chunk), :] = (first - second).astype(BF16)
-        atom = rows_like((chunk, HALO)) + base
-        for face in range(FACES):
-            hit = jnp.where(atom == halo[face : face + 1, :], 1.0, 0.0)
-            onehot[pl.ds(base, chunk), face * HALO : (face + 1) * HALO] = hit.astype(BF16)
+        sign = jnp.where(atom == bonds[0:1, :], 1.0, jnp.where(atom == bonds[1:2, :], -1.0, 0.0))
+        incid[pl.ds(base, chunk), :] = sign.astype(BF16)
         return 0
 
     lax.fori_loop(0, ATOMS // chunk, build, 0)
@@ -150,11 +146,6 @@
     own_hit = jnp.where((tile_of == slots[0:1, :]) & (slot_lane < count[0, 0]), 1.0, 0.0).astype(BF16)
     partner_hit = jnp.where(rows_like((32, 2 * TILE)) == slots[1:2, :], 1.0, 0.0).astype(BF16)
     mult[...] = lax.dot_general(partner_hit, own_hit, (((1,), (1,)), ((), ())), preferred_element_type=F32)
-
-    arrivals = exists[0].astype(jnp.int32)
-    for face in range(1, FACES):
-        arrivals = arrivals + exists[face].astype(jnp.int32)
-    pl.semaphore_wait(barrier, arrivals)
 
     face_row = rows_like((8, HALO))
 
@@ -168,26 +159,50 @@
             device_id_type=MESH,
         )
 
-    def short_blocks(first, last, acc):
-        def one_block(b, acc):
-            base = pl.multiple_of(b * BLOCK, BLOCK)
-            near[:, 0 : ATOMS + 3 * TILE] = jnp.dot(
-                left[pl.ds(base, BLOCK), :], right[:, 0 : ATOMS + 3 * TILE], preferred_element_type=F32
-            )
-
-            def group(g, acc):
-                at = pl.ds(pl.multiple_of(g * 8, 8), 8)
-                xj = [near[at, ATOMS + c * TILE : ATOMS + (c + 1) * TILE] for c in range(3)]
-                out = []
-                for t in range(OWN_TILES):
-                    n = jnp.maximum(near[at, t * TILE : (t + 1) * TILE], 0.0)
-                    s, fx, fy, fz = acc[4 * t : 4 * t + 4]
-                    out += [s + n, fx + n * xj[0], fy + n * xj[1], fz + n * xj[2]]
-                return tuple(out)
-
-            return lax.fori_loop(0, BLOCK // 8, group, acc, unroll=8)
-
-        return lax.fori_loop(first, last, one_block, acc)
+    half = 2 * TILE
+
+    def spread_rows(at, features):
+        for f in features:
+            cols = slice(f * TILE, (f + 1) * TILE)
+            from_cols = slice(ATOMS + f * TILE, ATOMS + (f + 1) * TILE)
+            spread[at, cols] = jnp.dot(left[at, :], right[:, from_cols], preferred_element_type=F32)
+
+    def short_sum(base, count, acc):
+        acc = list(acc)
+        partners = left[pl.ds(base, count), :]
+        for h in range(ATOMS // half):
+            near = jnp.dot(partners, right[:, h * half : (h + 1) * half], preferred_element_type=F32)
+            for g in range(count // 8):
+                xj = [spread[pl.ds(base + 8 * g, 8), c * TILE : (c + 1) * TILE] for c in range(3)]
+                for t in (2 * h, 2 * h + 1):
+                    col = (t - 2 * h) * TILE
+                    n = jnp.maximum(near[8 * g : 8 * g + 8, col : col + TILE], 0.0)
+                    acc[4 * t] = acc[4 * t] + n
+                    for c in range(3):
+                        acc[4 * t + 1 + c] = acc[4 * t + 1 + c] + n * xj[c]
+        return tuple(acc)
+
+    def chosen(source, index):
+        low = jnp.broadcast_to(index & (TILE - 1), (8, TILE))
+        tile = jnp.broadcast_to(index >> 7, (8, TILE))
+        out = jnp.zeros((8, TILE), F32)
+        for t in range(OWN_TILES):
+            cols = source[:, t * TILE : (t + 1) * TILE]
+            out = jnp.where(tile == t, jnp.take_along_axis(cols, low, axis=1, mode="promise_in_bounds"), out)
+        return out
+
+    def advance():
+        v = v_ref[...] + (0.5 * STEP) * mass * f_ref[...]
+        x = x_ref[...] + STEP * v
+        v_ref[...] = v
+        x_ref[...] = x
+        return jnp.where(row == 3, charge[...], x)
+
+    def export(k, source):
+        for face in range(FACES):
+            for part in range(HALO // TILE):
+                cols = slice(part * TILE, (part + 1) * TILE)
+                send[k, face, :, cols] = chosen(source, halo[face : face + 1, cols])
 
     def gathered(acc, x):
         parts = []
@@ -200,56 +215,85 @@
 
     zero_acc = tuple(jnp.zeros((8, TILE), F32) for _ in range(4 * OWN_TILES))
 
+    odd_x, odd_z = lax.rem(place[0], 2), lax.rem(place[2], 2)
+    far_x = (place[0] > 0) & (place[0] < extent[0] - 1)
+    far_z = (place[2] > 0) & (place[2] < extent[2] - 1)
+    arrivals_in_order = (
+        (1, 2, exists[2], False),
+        (1, 3, exists[3], False),
+        (0, 1 - odd_x, None, True),
+        (2, 5 - odd_z, None, True),
+        (0, odd_x, far_x, False),
+        (2, 4 + odd_z, far_z, False),
+    )
+
+    def absorb(k, axis, face, there, always):
+        def landed():
+            pltpu.make_async_remote_copy(
+                src_ref=send.at[k, face],
+                dst_ref=recv.at[k, face],
+                send_sem=send_sem.at[k, face],
+                recv_sem=recv_sem.at[k, face],
+                device_id=target[2 * axis],
+                device_id_type=MESH,
+            ).wait_recv()
+
+        if always:
+            landed()
+        else:
+            pl.when(there)(landed)
+        got = recv[k, face]
+        shift = jnp.asarray(2 * lax.rem(face, 2) - 1, F32) * SIDE
+        moved = got + jnp.where(face_row == axis, shift, 0.0)
+        if always:
+            block = featured(moved, got[3:4, :])
+        else:
+            seen = jnp.where(there, jnp.ones((8, HALO), F32), 0.0) > 0.0
+            moved = jnp.where(seen, moved, 0.0)
+            block = featured(moved, moved[3:4, :])
+            block = jnp.where(seen | (face_row != 3), block, FAR)
+        base = pl.multiple_of(ATOMS + face * HALO, HALO)
+        left[pl.ds(base, HALO), :] = left_rows(block).T.astype(BF16)
+        spread_rows(pl.ds(base, HALO), (0, 1, 2))
+
+    export(0, advance())
+
+    arrivals = exists[0].astype(jnp.int32)
+    for face in range(1, FACES):
+        arrivals = arrivals + exists[face].astype(jnp.int32)
+    pl.semaphore_wait(barrier, arrivals)
+
     def inner(k, _):
-        v = v_ref[...] + (0.5 * STEP) * mass * f_ref[...]
-        x = x_ref[...] + STEP * v
-        v_ref[...] = v
-        x_ref[...] = x
-        features = featured(x, charge[...])
-        rows = left_rows(features)
-        high, mid, low = rows[0:8], rows[24:32], rows[40:48]
-        parts = jnp.concatenate([high, mid, low], axis=0).astype(BF16)
-
-        picked = jnp.dot(parts, onehot[...], preferred_element_type=F32)
-        picked = picked[0:8] + picked[8:16] + picked[16:24]
-        for face in range(FACES):
-            send[k, face] = picked[:, face * HALO : (face + 1) * HALO]
         for face in range(FACES):
 
             @pl.when(exists[face])
             def _(face=face):
                 copy_out(k, face).start()
 
+        x = x_ref[...]
+        features = featured(x, charge[...])
+        rows = left_rows(features)
         left[0:ATOMS, :] = rows.T.astype(BF16)
         right[:, 0:ATOMS] = right_rows(partner_side(features, SHORT_INV)).astype(BF16)
-
+        spread_rows(slice(0, ATOMS), (0, 1, 2))
+
+        parts = jnp.concatenate([rows[0:8], rows[24:32], rows[40:48]], axis=0).astype(BF16)
         apart = jnp.dot(parts, incid[...], preferred_element_type=F32)
         apart = apart[0:8] + apart[8:16] + apart[16:24]
-        pull = split3(bond_k[...] * apart)
+        pull = split3(stiff * apart)
         pull = jnp.concatenate(pull, axis=0).astype(BF16)
         drawn = lax.dot_general(pull, incid[...], (((1,), (1,)), ((), ())), preferred_element_type=F32)
         f_ref[...] = -(drawn[0:8] + drawn[8:16] + drawn[16:24])
 
-        acc = short_blocks(0, ATOMS // BLOCK, zero_acc)
-
-        for face in range(FACES):
-
-            @pl.when(exists[face])
-            def _(face=face):
-                copy_out(k, face ^ 1).wait_recv()
-
-        for face in range(FACES):
-            axis = face // 2
-            shift = SIDE if face % 2 else -SIDE
-            got = recv[k, face]
-            seen = jnp.where(exists[face], jnp.ones((8, HALO), F32), 0.0) > 0.0
-            moved = jnp.where(seen, got + jnp.where(face_row == axis, shift, 0.0), 0.0)
-            there = featured(moved, moved[5:6, :])
-            there = jnp.where(seen | (face_row != 3), there, FAR)
-            base = ATOMS + face * HALO
-            left[base : base + HALO, :] = left_rows(there).T.astype(BF16)
-
-        acc = short_blocks(ATOMS // BLOCK, VISIBLE // BLOCK, acc)
+        acc = short_sum(0, ATOMS, zero_acc)
+
+        for pair in range(FACES // 2):
+            now = arrivals_in_order[2 * pair : 2 * pair + 2]
+            for axis, face, there, always in now:
+                absorb(k, axis, face, there, always)
+            for axis, face, there, always in now:
+                acc = short_sum(pl.multiple_of(ATOMS + face * HALO, HALO), HALO, acc)
+
         force = f_ref[...] + SHORT_SCALE * gathered(acc, x)
         force = jnp.where(row < 3, force, 0.0)
         f_ref[...] = force
@@ -261,6 +305,10 @@
             def _(face=face):
                 copy_out(k, face).wait_send()
 
+        @pl.when(k < INNER - 1)
+        def _():
+            export(k + 1, advance())
+
         return 0
 
     lax.fori_loop(0, INNER, inner, 0)
@@ -268,32 +316,27 @@
     x = x_ref[...]
     features = featured(x, charge[...])
     right[:, 0:ATOMS] = right_rows(partner_side(features, LONG_INV)).astype(BF16)
-    total[...] = jnp.zeros_like(total)
-
-    def long_block(b, _):
-        base = pl.multiple_of(b * TILE, TILE)
-        near[0:TILE, :] = jnp.dot(left[pl.ds(base, TILE), :], right[...], preferred_element_type=F32)
-
-        def group(g, acc):
-            at = pl.ds(pl.multiple_of(g * 8, 8), 8)
-            xj = [near[at, ATOMS + c * TILE : ATOMS + (c + 1) * TILE] for c in range(4)]
-            out = []
-            for t in range(OWN_TILES):
-                n = jnp.maximum(near[at, t * TILE : (t + 1) * TILE], 0.0) * xj[3]
-                s, fx, fy, fz = acc[4 * t : 4 * t + 4]
-                out += [s + n, fx + n * xj[0], fy + n * xj[1], fz + n * xj[2]]
-            return tuple(out)
-
-        acc = lax.fori_loop(0, TILE // 8, group, zero_acc, unroll=8)
-        times = mult[pl.ds(b, 1), :]
-        for t in range(OWN_TILES):
-            m = times[:, t * TILE : (t + 1) * TILE]
-            for c in range(4):
-                total[4 * t + c] = total[4 * t + c] + m * acc[4 * t + c]
-        return 0
-
-    lax.fori_loop(0, VISIBLE // TILE, long_block, 0)
-    acc = [total[i] for i in range(4 * OWN_TILES)]
+    spread_rows(slice(0, VISIBLE), (3,))
+    acc = []
+    for h in range(ATOMS // half):
+        total = [jnp.zeros((8, TILE), F32) for _ in range(8)]
+        for u in range(VISIBLE // TILE):
+            partners = left[u * TILE : (u + 1) * TILE, :]
+            near = jnp.dot(partners, right[:, h * half : (h + 1) * half], preferred_element_type=F32)
+            part = [jnp.zeros((8, TILE), F32) for _ in range(8)]
+            for g in range(TILE // 8):
+                at = slice(u * TILE + 8 * g, u * TILE + 8 * g + 8)
+                xj = [spread[at, c * TILE : (c + 1) * TILE] for c in range(4)]
+                for t in range(2):
+                    n = jnp.maximum(near[8 * g : 8 * g + 8, t * TILE : (t + 1) * TILE], 0.0) * xj[3]
+                    part[4 * t] = part[4 * t] + n
+                    for c in range(3):
+                        part[4 * t + 1 + c] = part[4 * t + 1 + c] + n * xj[c]
+            for t in range(2):
+                m = mult[u : u + 1, h * half + t * TILE : h * half + (t + 1) * TILE]
+                for c in range(4):
+                    total[4 * t + c] = total[4 * t + c] + m * part[4 * t + c]
+        acc += total
     slow_now = LONG_SCALE * charge[...] * gathered(acc, x)
     slow_out[...] = slow_now[0:3, :]
     fast_out[...] = f_ref[0:3, :]
@@ -319,11 +362,9 @@
             pltpu.VMEM((INNER, FACES, 8, HALO), F32),
             pltpu.VMEM((VISIBLE, KDIM), BF16),
             pltpu.VMEM((KDIM, ATOMS + 4 * TILE), BF16),
-            pltpu.VMEM((BLOCK, ATOMS + 4 * TILE), F32),
+            pltpu.VMEM((VISIBLE, 4 * TILE), F32),
             pltpu.VMEM((ATOMS, ATOMS), BF16),
-            pltpu.VMEM((ATOMS, FACES * HALO), BF16),
             pltpu.VMEM((32, ATOMS), F32),
-            pltpu.VMEM((4 * OWN_TILES, 8, TILE), F32),
             pltpu.VMEM((8, 2 * TILE), jnp.int32),
             pltpu.SemaphoreType.DMA((INNER, FACES)),
             pltpu.SemaphoreType.DMA((INNER, FACES)),

time: 53.9 us -> 39.8 us (0.74)
  the two profiles are of different devices: /device:TPU:1 before, /device:TPU:75 now
where the time goes in v2:
time: 39.8 us; the launch traced here: 39.4 us
  Pallas kernels  34.7 us (87%)
  local copies, waits for them, and re-layouts  3.39 us (9%)
  between operations  1.3 us (3%)
    pallas_call x1, Pallas kernels, on_device(): pl.pallas_call(kernel, out_shape=(out, out, out, out), in_specs=[vmem] *...  34.7 us
    unnamed x10, local copies, waits for them, and re-layouts  3.39 us

profile of v2, /device:TPU:75, one launch (start us, length us, event | category | flops | bytes accessed | tf_op | source)
XLA Modules:
  0.0 39.4 jit_solution(8428715594820178967)
XLA Ops:
  1.3 34.7 %outer_step.1 = (f32[3,1024]{1,0:T(4,128)}, f32[3,1024]{1,0:T(4,128)}, f32[3,1024]{1,0:T(4,128)}, f32[3,1024]{1,0:T(4,128)}) custom-call(f32[3,1024]{1,0:T(4,128)} %pos.1, f32[3,1024]{1,0:T(4,128)} %vel.1, f32[1,1024]{1,0:T(1,128)} %bitcast.7, f32[1,1024]{1,0:T(1,128)} %bitcast.8, f32[3,1024]{1,0:T(4,128)} %fast.1, f32[3,1024]{1,0:T(4,128)} %slow.1, ...), custom_call_target="tpu_custom_call" | custom-call | tf_op jit(solution)/shard_map/outer_step/pallas_call | solution.py:351
  36.0 0.0 copy-start.2
  36.0 1.3 %copy.21 = f32[3,1024]{1,0:T(4,128)} copy(f32[3,1024]{1,0:T(4,128)} %get-tuple-element.8) | data formatting | bytes 24576
  37.3 0.0 copy-done.2
  37.3 0.0 copy-start.1
  37.3 0.6 %copy.22 = f32[3,1024]{1,0:T(4,128)} copy(f32[3,1024]{1,0:T(4,128)S(1)} %copy-done.2) | data formatting | bytes 24576
  37.9 0.1 copy-done.1
  38.1 0.0 copy-start
  38.1 0.6 %copy.23 = f32[3,1024]{1,0:T(4,128)} copy(f32[3,1024]{1,0:T(4,128)S(1)} %copy-done.1) | data formatting | bytes 24576
  38.7 0.1 copy-done
  38.8 0.6 %copy.24 = f32[3,1024]{1,0:T(4,128)} copy(f32[3,1024]{1,0:T(4,128)S(1)} %copy-done) | data formatting | bytes 24576
Async XLA Ops:
  36.0 1.3 %copy-start.2 = (f32[3,1024]{1,0:T(4,128)S(1)}, f32[3,1024]{1,0:T(4,128)}, u32[]{:S(2)}) copy-start(f32[3,1024]{1,0:T(4,128)} %get-tuple-element.9) | copy-start | bytes 36868
  37.3 0.7 %copy-start.1 = (f32[3,1024]{1,0:T(4,128)S(1)}, f32[3,1024]{1,0:T(4,128)}, u32[]{:S(2)}) copy-start(f32[3,1024]{1,0:T(4,128)} %get-tuple-element.10) | copy-start | bytes 36868
  38.1 0.7 %copy-start = (f32[3,1024]{1,0:T(4,128)S(1)}, f32[3,1024]{1,0:T(4,128)}, u32[]{:S(2)}) copy-start(f32[3,1024]{1,0:T(4,128)} %get-tuple-element.11) | copy-start | bytes 36868

commit v3 on v2

--- a/solution.py
+++ b/solution.py
@@ -30,6 +30,7 @@
 OWN_TILES = ATOMS // TILE
 SLOTS = 192
 AXES = ("gx", "gy", "gz")
+GROUPS = (ATOMS, HALO, 3 * HALO, 2 * HALO)
 
 
 def rows_like(shape):
@@ -86,12 +87,15 @@
     return out
 
 
-def kernel(
-    pos, vel, inv_mass, charge, fast, slow, bonds, bond_k, halo, own_slot, partner_slot, count,
-    disp_out, vel_out, fast_out, slow_out,
-    x_ref, v_ref, f_ref, start_ref, send, recv, left, right, spread, incid, mult, slots,
-    send_sem, recv_sem,
-):
+def kernel(*refs):
+    sources, count, packed_out, landing = refs[:11], refs[11], refs[12], refs[13]
+    x_ref, v_ref, f_ref, start_ref, send, recv, lefts, spreads, right, incid, mult, slots = refs[14:26]
+    send_sem, recv_sem, load_sem = refs[26:]
+    pos, vel, inv_mass, charge, fast, slow, bonds, bond_k, halo, own_slot, partner_slot = landing
+    loads = [pltpu.make_async_copy(a, b, load_sem.at[i]) for i, (a, b) in enumerate(zip(sources, landing))]
+    for load in loads:
+        load.start()
+
     place = [lax.axis_index(a) for a in AXES]
     extent = [lax.axis_size(a) for a in AXES]
     exists = []
@@ -109,6 +113,9 @@
         @pl.when(exists[face])
         def _(face=face):
             pl.semaphore_signal(barrier, inc=1, device_id=target[face], device_id_type=MESH)
+
+    for load in loads:
+        load.wait()
 
     wide = (8, ATOMS)
     row = rows_like(wide)
@@ -161,25 +168,32 @@
 
     half = 2 * TILE
 
-    def spread_rows(at, features):
+    def spread_rows(group, at, features):
         for f in features:
             cols = slice(f * TILE, (f + 1) * TILE)
             from_cols = slice(ATOMS + f * TILE, ATOMS + (f + 1) * TILE)
-            spread[at, cols] = jnp.dot(left[at, :], right[:, from_cols], preferred_element_type=F32)
-
-    def short_sum(base, count, acc):
+            spreads[group][at, cols] = jnp.dot(
+                lefts[group][at, :], right[:, from_cols], preferred_element_type=F32
+            )
+
+    def short_sum(group, base, acc, beside=()):
         acc = list(acc)
-        partners = left[pl.ds(base, count), :]
+        beside = list(beside)
+        partners = lefts[group][base : base + BLOCK, :]
         for h in range(ATOMS // half):
             near = jnp.dot(partners, right[:, h * half : (h + 1) * half], preferred_element_type=F32)
-            for g in range(count // 8):
-                xj = [spread[pl.ds(base + 8 * g, 8), c * TILE : (c + 1) * TILE] for c in range(3)]
+            if beside:
+                beside.pop(0)()
+            for g in range(BLOCK // 8):
+                at = slice(base + 8 * g, base + 8 * g + 8)
+                xj = [spreads[group][at, c * TILE : (c + 1) * TILE] for c in range(3)]
                 for t in (2 * h, 2 * h + 1):
                     col = (t - 2 * h) * TILE
                     n = jnp.maximum(near[8 * g : 8 * g + 8, col : col + TILE], 0.0)
                     acc[4 * t] = acc[4 * t] + n
                     for c in range(3):
                         acc[4 * t + 1 + c] = acc[4 * t + 1 + c] + n * xj[c]
+        assert not beside
         return tuple(acc)
 
     def chosen(source, index):
@@ -218,17 +232,14 @@
     odd_x, odd_z = lax.rem(place[0], 2), lax.rem(place[2], 2)
     far_x = (place[0] > 0) & (place[0] < extent[0] - 1)
     far_z = (place[2] > 0) & (place[2] < extent[2] - 1)
-    arrivals_in_order = (
-        (1, 2, exists[2], False),
-        (1, 3, exists[3], False),
-        (0, 1 - odd_x, None, True),
-        (2, 5 - odd_z, None, True),
-        (0, odd_x, far_x, False),
-        (2, 4 + odd_z, far_z, False),
+    groups = (
+        ((2, 5 - odd_z, None),),
+        ((1, 2, exists[2]), (1, 3, exists[3]), (0, 1 - odd_x, None)),
+        ((0, odd_x, far_x), (2, 4 + odd_z, far_z)),
     )
 
-    def absorb(k, axis, face, there, always):
-        def landed():
+    def landed(k, axis, face, there):
+        def wait():
             pltpu.make_async_remote_copy(
                 src_ref=send.at[k, face],
                 dst_ref=recv.at[k, face],
@@ -238,23 +249,26 @@
                 device_id_type=MESH,
             ).wait_recv()
 
-        if always:
-            landed()
+        if there is None:
+            wait()
         else:
-            pl.when(there)(landed)
+            pl.when(there)(wait)
+
+    def absorb(k, group, i):
+        axis, face, there = groups[group - 1][i]
         got = recv[k, face]
         shift = jnp.asarray(2 * lax.rem(face, 2) - 1, F32) * SIDE
         moved = got + jnp.where(face_row == axis, shift, 0.0)
-        if always:
+        if there is None:
             block = featured(moved, got[3:4, :])
         else:
             seen = jnp.where(there, jnp.ones((8, HALO), F32), 0.0) > 0.0
             moved = jnp.where(seen, moved, 0.0)
             block = featured(moved, moved[3:4, :])
             block = jnp.where(seen | (face_row != 3), block, FAR)
-        base = pl.multiple_of(ATOMS + face * HALO, HALO)
-        left[pl.ds(base, HALO), :] = left_rows(block).T.astype(BF16)
-        spread_rows(pl.ds(base, HALO), (0, 1, 2))
+        at = slice(i * HALO, (i + 1) * HALO)
+        lefts[group][at, :] = left_rows(block).T.astype(BF16)
+        spread_rows(group, at, (0, 1, 2))
 
     export(0, advance())
 
@@ -273,26 +287,53 @@
         x = x_ref[...]
         features = featured(x, charge[...])
         rows = left_rows(features)
-        left[0:ATOMS, :] = rows.T.astype(BF16)
         right[:, 0:ATOMS] = right_rows(partner_side(features, SHORT_INV)).astype(BF16)
-        spread_rows(slice(0, ATOMS), (0, 1, 2))
-
         parts = jnp.concatenate([rows[0:8], rows[24:32], rows[40:48]], axis=0).astype(BF16)
-        apart = jnp.dot(parts, incid[...], preferred_element_type=F32)
-        apart = apart[0:8] + apart[8:16] + apart[16:24]
-        pull = split3(stiff * apart)
-        pull = jnp.concatenate(pull, axis=0).astype(BF16)
-        drawn = lax.dot_general(pull, incid[...], (((1,), (1,)), ((), ())), preferred_element_type=F32)
-        f_ref[...] = -(drawn[0:8] + drawn[8:16] + drawn[16:24])
-
-        acc = short_sum(0, ATOMS, zero_acc)
-
-        for pair in range(FACES // 2):
-            now = arrivals_in_order[2 * pair : 2 * pair + 2]
-            for axis, face, there, always in now:
-                absorb(k, axis, face, there, always)
-            for axis, face, there, always in now:
-                acc = short_sum(pl.multiple_of(ATOMS + face * HALO, HALO), HALO, acc)
+
+        def own(i):
+            at = slice(i * BLOCK, (i + 1) * BLOCK)
+            lefts[0][at, :] = rows[:, at].T.astype(BF16)
+            spread_rows(0, at, (0, 1, 2))
+
+        pulls = []
+
+        def pull(i):
+            at = slice(i * BLOCK, (i + 1) * BLOCK)
+            apart = jnp.dot(parts, incid[:, at], preferred_element_type=F32)
+            apart = stiff[:, at] * (apart[0:8] + apart[8:16] + apart[16:24])
+            pulls.append(jnp.concatenate(split3(apart), axis=0).astype(BF16))
+
+        def draw(i):
+            at = slice(i * BLOCK, (i + 1) * BLOCK)
+            pulled = jnp.concatenate(pulls, axis=1)
+            drawn = lax.dot_general(
+                pulled, incid[at, :], (((1,), (1,)), ((), ())), preferred_element_type=F32
+            )
+            f_ref[:, at] = -(drawn[0:8] + drawn[8:16] + drawn[16:24])
+
+        def do(work, *what):
+            return functools.partial(work, *what)
+
+        own(0)
+        acc = short_sum(0, 0, zero_acc, (do(own, 1), do(pull, 0), do(pull, 1)))
+        acc = short_sum(0, BLOCK, acc, (do(own, 2), do(pull, 2), do(pull, 3)))
+
+        for item in groups[0]:
+            landed(k, *item)
+        acc = short_sum(0, 2 * BLOCK, acc, (do(own, 3), do(absorb, k, 1, 0), do(draw, 0), do(draw, 1)))
+        acc = short_sum(0, 3 * BLOCK, acc, (do(draw, 2), do(draw, 3)))
+
+        for item in groups[1]:
+            landed(k, *item)
+        acc = short_sum(1, 0, acc, (do(absorb, k, 2, 0), do(absorb, k, 2, 1), do(absorb, k, 2, 2)))
+
+        for item in groups[2]:
+            landed(k, *item)
+        acc = short_sum(2, 0, acc, (do(absorb, k, 3, 0), do(absorb, k, 3, 1)))
+        acc = short_sum(2, BLOCK, acc)
+        acc = short_sum(2, 2 * BLOCK, acc)
+        acc = short_sum(3, 0, acc)
+        acc = short_sum(3, BLOCK, acc)
 
         force = f_ref[...] + SHORT_SCALE * gathered(acc, x)
         force = jnp.where(row < 3, force, 0.0)
@@ -316,65 +357,98 @@
     x = x_ref[...]
     features = featured(x, charge[...])
     right[:, 0:ATOMS] = right_rows(partner_side(features, LONG_INV)).astype(BF16)
-    spread_rows(slice(0, VISIBLE), (3,))
+    tiles = [(0, i, i) for i in range(OWN_TILES)]
+    for group in (1, 2, 3):
+        for i, (axis, face, there) in enumerate(groups[group - 1]):
+            tiles += [(group, 2 * i + part, OWN_TILES + 2 * face + part) for part in range(2)]
+
+    def spread_charge(at):
+        if at < len(tiles):
+            group, u, _ = tiles[at]
+            spread_rows(group, slice(u * TILE, (u + 1) * TILE), (3,))
+
+    spread_charge(0)
     acc = []
     for h in range(ATOMS // half):
         total = [jnp.zeros((8, TILE), F32) for _ in range(8)]
-        for u in range(VISIBLE // TILE):
-            partners = left[u * TILE : (u + 1) * TILE, :]
+        for at_tile, (group, u, number) in enumerate(tiles):
+            partners = lefts[group][u * TILE : (u + 1) * TILE, :]
             near = jnp.dot(partners, right[:, h * half : (h + 1) * half], preferred_element_type=F32)
+            if h == 0:
+                spread_charge(at_tile + 1)
             part = [jnp.zeros((8, TILE), F32) for _ in range(8)]
             for g in range(TILE // 8):
                 at = slice(u * TILE + 8 * g, u * TILE + 8 * g + 8)
-                xj = [spread[at, c * TILE : (c + 1) * TILE] for c in range(4)]
+                xj = [spreads[group][at, c * TILE : (c + 1) * TILE] for c in range(4)]
                 for t in range(2):
                     n = jnp.maximum(near[8 * g : 8 * g + 8, t * TILE : (t + 1) * TILE], 0.0) * xj[3]
                     part[4 * t] = part[4 * t] + n
                     for c in range(3):
                         part[4 * t + 1 + c] = part[4 * t + 1 + c] + n * xj[c]
+            times = mult[pl.ds(number, 1), h * half : (h + 1) * half]
             for t in range(2):
-                m = mult[u : u + 1, h * half + t * TILE : h * half + (t + 1) * TILE]
+                m = times[:, t * TILE : (t + 1) * TILE]
                 for c in range(4):
                     total[4 * t + c] = total[4 * t + c] + m * part[4 * t + c]
         acc += total
     slow_now = LONG_SCALE * charge[...] * gathered(acc, x)
-    slow_out[...] = slow_now[0:3, :]
-    fast_out[...] = f_ref[0:3, :]
-    disp_out[...] = (x - start_ref[...])[0:3, :]
-    vel_out[...] = v_ref[0:3, :] + (0.5 * INNER * STEP) * mass * slow_now[0:3, :]
+    packed_out[0:8, :] = x - start_ref[...]
+    packed_out[8:16, :] = v_ref[...] + (0.5 * INNER * STEP) * mass * slow_now
+    packed_out[16:24, :] = f_ref[...]
+    packed_out[24:32, :] = slow_now
+
+
+def finish(packed, disp_out, vel_out, fast_out, slow_out):
+    disp_out[...] = packed[0:3, :]
+    vel_out[...] = packed[8:11, :]
+    fast_out[...] = packed[16:19, :]
+    slow_out[...] = packed[24:27, :]
 
 
 def on_device(pos, vel, inv_mass, charge, fast, slow, bonds, bond_k, halo, own_slot, partner_slot, count):
     vmem = pl.BlockSpec(memory_space=pltpu.VMEM)
     smem = pl.BlockSpec(memory_space=pltpu.SMEM)
     out = jax.ShapeDtypeStruct((3, ATOMS), F32)
-    return pl.pallas_call(
+    arrays = (
+        pos, vel, inv_mass[None, :], charge[None, :], fast, slow, bonds, bond_k[None, :], halo,
+        own_slot[None, :], partner_slot[None, :],
+    )
+    packed = pl.pallas_call(
         kernel,
-        out_shape=(out, out, out, out),
-        in_specs=[vmem] * 11 + [smem],
-        out_specs=(vmem,) * 4,
+        out_shape=jax.ShapeDtypeStruct((32, ATOMS), F32),
+        in_specs=[pl.BlockSpec(memory_space=pltpu.HBM)] * 11 + [smem],
+        out_specs=vmem,
         scratch_shapes=[
+            [pltpu.VMEM(a.shape, a.dtype) for a in arrays],
             pltpu.VMEM((8, ATOMS), F32),
             pltpu.VMEM((8, ATOMS), F32),
             pltpu.VMEM((8, ATOMS), F32),
             pltpu.VMEM((8, ATOMS), F32),
             pltpu.VMEM((INNER, FACES, 8, HALO), F32),
             pltpu.VMEM((INNER, FACES, 8, HALO), F32),
-            pltpu.VMEM((VISIBLE, KDIM), BF16),
+            [pltpu.VMEM((count, KDIM), BF16) for count in GROUPS],
+            [pltpu.VMEM((count, 4 * TILE), F32) for count in GROUPS],
             pltpu.VMEM((KDIM, ATOMS + 4 * TILE), BF16),
-            pltpu.VMEM((VISIBLE, 4 * TILE), F32),
             pltpu.VMEM((ATOMS, ATOMS), BF16),
             pltpu.VMEM((32, ATOMS), F32),
             pltpu.VMEM((8, 2 * TILE), jnp.int32),
             pltpu.SemaphoreType.DMA((INNER, FACES)),
             pltpu.SemaphoreType.DMA((INNER, FACES)),
+            pltpu.SemaphoreType.DMA((11,)),
         ],
-        compiler_params=pltpu.CompilerParams(collective_id=0, has_side_effects=True),
+        compiler_params=pltpu.CompilerParams(
+            collective_id=0, has_side_effects=True
+        ),
         name="outer_step",
-    )(
-        pos, vel, inv_mass[None, :], charge[None, :], fast, slow, bonds, bond_k[None, :], halo,
-        own_slot[None, :], partner_slot[None, :], count[None, :],
-    )
+    )(*arrays, count[None, :])
+    return pl.pallas_call(
+        finish,
+        out_shape=(out, out, out, out),
+        in_specs=[vmem],
+        out_specs=(vmem,) * 4,
+
+        name="finish",
+    )(packed)
 
 
 def solution(mesh):

time: 39.8 us -> 35.5 us (0.89)
  the two profiles are of different devices: /device:TPU:75 before, /device:TPU:1 now
where the time goes in v3:
time: 35.5 us; the launch traced here: 35.3 us
  Pallas kernels  34 us (96%)
  between operations  1.29 us (4%)
    pallas_call x1, Pallas kernels, on_device(): pl.pallas_call(kernel, out_shape=jax.ShapeDtypeStruct((32, ATOMS), F32),...  32.5 us
    pallas_call x1, Pallas kernels, on_device(): pl.pallas_call(finish, out_shape=(out, out, out, out), in_specs=[vmem], o...  1.54 us

profile of v3, /device:TPU:1, one launch (start us, length us, event | category | flops | bytes accessed | tf_op | source)
XLA Modules:
  0.0 35.3 jit_solution(15479518681912994352)
XLA Ops:
  1.3 32.5 %outer_step.1.packed = f32[32,1024]{1,0:T(8,128)} custom-call(f32[3,1024]{1,0:T(4,128)} %refs_0_.1, f32[3,1024]{1,0:T(4,128)} %refs_1_.1, f32[1,1024]{1,0:T(1,128)} %bitcast.7, f32[1,1024]{1,0:T(1,128)} %bitcast.8, f32[3,1024]{1,0:T(4,128)} %refs_4_.1, f32[3,1024]{1,0:T(4,128)} %refs_5_.1, s32[2,1024]{1,0:T(2,128)} %refs_6_.1, f32[1,1024]{1,0:T(1,128)} %bitcast.9, ...), custom_call_target="tpu_custom_call" | custom-call | tf_op jit(solution)/shard_map/outer_step/pallas_call | solution.py:416
  33.8 1.5 %finish.1 = (f32[3,1024]{1,0:T(4,128)}, f32[3,1024]{1,0:T(4,128)}, f32[3,1024]{1,0:T(4,128)}, f32[3,1024]{1,0:T(4,128)}) custom-call(f32[32,1024]{1,0:T(8,128)} %outer_step.1.packed), custom_call_target="tpu_custom_call" | custom-call | tf_op jit(solution)/shard_map/finish/pallas_call | solution.py:444

commit v4 on v3

--- a/solution.py
+++ b/solution.py
@@ -132,39 +132,25 @@
     start_ref[...] = x_ref[...]
 
     stiff = jnp.where(bonds[0:1, :] == bonds[1:2, :], 0.0, bond_k[...])
-    chunk = 128
-
-    def build(c, _):
-        base = pl.multiple_of(c * chunk, chunk)
-        atom = rows_like((chunk, ATOMS)) + base
-        sign = jnp.where(atom == bonds[0:1, :], 1.0, jnp.where(atom == bonds[1:2, :], -1.0, 0.0))
-        incid[pl.ds(base, chunk), :] = sign.astype(BF16)
-        return 0
-
-    lax.fori_loop(0, ATOMS // chunk, build, 0)
-
-    right[:, ATOMS : ATOMS + 4 * TILE] = pick_rows((0, 1, 2, 5)).astype(BF16)
-
-    slots[...] = jnp.full(slots.shape, -1, jnp.int32)
-    slots[0:1, 0:SLOTS] = own_slot[...]
-    slots[1:2, 0:SLOTS] = partner_slot[...]
-    slot_lane = lanes_like((ATOMS, 2 * TILE))
-    tile_of = rows_like((ATOMS, 2 * TILE)) // TILE
-    own_hit = jnp.where((tile_of == slots[0:1, :]) & (slot_lane < count[0, 0]), 1.0, 0.0).astype(BF16)
-    partner_hit = jnp.where(rows_like((32, 2 * TILE)) == slots[1:2, :], 1.0, 0.0).astype(BF16)
-    mult[...] = lax.dot_general(partner_hit, own_hit, (((1,), (1,)), ((), ())), preferred_element_type=F32)
-
     face_row = rows_like((8, HALO))
 
-    def copy_out(k, face):
+    def copy_out(k, axis, face):
+        side = lax.rem(face, 2)
+        over = face + 1 - 2 * side
         return pltpu.make_async_remote_copy(
             src_ref=send.at[k, face],
-            dst_ref=recv.at[k, face ^ 1],
+            dst_ref=recv.at[k, over],
             send_sem=send_sem.at[k, face],
-            recv_sem=recv_sem.at[k, face ^ 1],
-            device_id=target[face],
+            recv_sem=recv_sem.at[k, over],
+            device_id={AXES[axis]: place[axis] + 2 * side - 1},
             device_id_type=MESH,
         )
+
+    def when(there, action):
+        if there is None:
+            action()
+        else:
+            pl.when(there)(action)
 
     half = 2 * TILE
 
@@ -216,7 +202,7 @@
         for face in range(FACES):
             for part in range(HALO // TILE):
                 cols = slice(part * TILE, (part + 1) * TILE)
-                send[k, face, :, cols] = chosen(source, halo[face : face + 1, cols])
+                send[k, face, :, cols] = chosen(source, halo[face : face + 1, cols])[0:4, :]
 
     def gathered(acc, x):
         parts = []
@@ -249,14 +235,12 @@
                 device_id_type=MESH,
             ).wait_recv()
 
-        if there is None:
-            wait()
-        else:
-            pl.when(there)(wait)
+        when(there, wait)
 
     def absorb(k, group, i):
         axis, face, there = groups[group - 1][i]
         got = recv[k, face]
+        got = jnp.concatenate([got, jnp.zeros_like(got)], axis=0)
         shift = jnp.asarray(2 * lax.rem(face, 2) - 1, F32) * SIDE
         moved = got + jnp.where(face_row == axis, shift, 0.0)
         if there is None:
@@ -277,12 +261,34 @@
         arrivals = arrivals + exists[face].astype(jnp.int32)
     pl.semaphore_wait(barrier, arrivals)
 
+    def tables():
+        chunk = 128
+
+        def build(c, _):
+            base = pl.multiple_of(c * chunk, chunk)
+            atom = rows_like((chunk, ATOMS)) + base
+            sign = jnp.where(atom == bonds[0:1, :], 1.0, jnp.where(atom == bonds[1:2, :], -1.0, 0.0))
+            incid[pl.ds(base, chunk), :] = sign.astype(BF16)
+            return 0
+
+        lax.fori_loop(0, ATOMS // chunk, build, 0)
+
+        right[:, ATOMS : ATOMS + 4 * TILE] = pick_rows((0, 1, 2, 5)).astype(BF16)
+
+        slots[...] = jnp.full(slots.shape, -1, jnp.int32)
+        slots[0:1, 0:SLOTS] = own_slot[...]
+        slots[1:2, 0:SLOTS] = partner_slot[...]
+        slot_lane = lanes_like((ATOMS, 2 * TILE))
+        tile_of = rows_like((ATOMS, 2 * TILE)) // TILE
+        own_hit = jnp.where((tile_of == slots[0:1, :]) & (slot_lane < count[0, 0]), 1.0, 0.0).astype(BF16)
+        partner_hit = jnp.where(rows_like((32, 2 * TILE)) == slots[1:2, :], 1.0, 0.0).astype(BF16)
+        mult[...] = lax.dot_general(partner_hit, own_hit, (((1,), (1,)), ((), ())), preferred_element_type=F32)
+
     def inner(k, _):
-        for face in range(FACES):
-
-            @pl.when(exists[face])
-            def _(face=face):
-                copy_out(k, face).start()
+        for axis, face, there in groups[2] + groups[1] + groups[0]:
+            when(there, lambda axis=axis, face=face: copy_out(k, axis, face).start())
+
+        pl.when(k == 0)(tables)
 
         x = x_ref[...]
         features = featured(x, charge[...])
@@ -323,15 +329,18 @@
         acc = short_sum(0, 2 * BLOCK, acc, (do(own, 3), do(absorb, k, 1, 0), do(draw, 0), do(draw, 1)))
         acc = short_sum(0, 3 * BLOCK, acc, (do(draw, 2), do(draw, 3)))
 
+        for axis, face, there in groups[2] + groups[1] + groups[0]:
+            when(there, lambda axis=axis, face=face: copy_out(k, axis, face).wait_send())
         for item in groups[1]:
             landed(k, *item)
         acc = short_sum(1, 0, acc, (do(absorb, k, 2, 0), do(absorb, k, 2, 1), do(absorb, k, 2, 2)))
 
+        acc = short_sum(2, 0, acc)
+        acc = short_sum(2, BLOCK, acc)
+
         for item in groups[2]:
             landed(k, *item)
-        acc = short_sum(2, 0, acc, (do(absorb, k, 3, 0), do(absorb, k, 3, 1)))
-        acc = short_sum(2, BLOCK, acc)
-        acc = short_sum(2, 2 * BLOCK, acc)
+        acc = short_sum(2, 2 * BLOCK, acc, (do(absorb, k, 3, 0), do(absorb, k, 3, 1)))
         acc = short_sum(3, 0, acc)
         acc = short_sum(3, BLOCK, acc)
 
@@ -339,12 +348,6 @@
         force = jnp.where(row < 3, force, 0.0)
         f_ref[...] = force
         v_ref[...] = v_ref[...] + (0.5 * STEP) * mass * force
-
-        for face in range(FACES):
-
-            @pl.when(exists[face])
-            def _(face=face):
-                copy_out(k, face).wait_send()
 
         @pl.when(k < INNER - 1)
         def _():
@@ -415,7 +418,7 @@
     )
     packed = pl.pallas_call(
         kernel,
-        out_shape=jax.ShapeDtypeStruct((32, ATOMS), F32),
+        out_shape=pltpu.VMEM((32, ATOMS), F32),
         in_specs=[pl.BlockSpec(memory_space=pltpu.HBM)] * 11 + [smem],
         out_specs=vmem,
         scratch_shapes=[
@@ -424,8 +427,8 @@
             pltpu.VMEM((8, ATOMS), F32),
             pltpu.VMEM((8, ATOMS), F32),
             pltpu.VMEM((8, ATOMS), F32),
-            pltpu.VMEM((INNER, FACES, 8, HALO), F32),
-            pltpu.VMEM((INNER, FACES, 8, HALO), F32),
+            pltpu.VMEM((INNER, FACES, 4, HALO), F32),
+            pltpu.VMEM((INNER, FACES, 4, HALO), F32),
             [pltpu.VMEM((count, KDIM), BF16) for count in GROUPS],
             [pltpu.VMEM((count, 4 * TILE), F32) for count in GROUPS],
             pltpu.VMEM((KDIM, ATOMS + 4 * TILE), BF16),
@@ -447,6 +450,7 @@
         in_specs=[vmem],
         out_specs=(vmem,) * 4,
 
+        compiler_params=pltpu.CompilerParams(vmem_limit_bytes=4 * 1024 * 1024),
         name="finish",
     )(packed)
 

time: 35.5 us -> 33.2 us (0.935)
  Pallas kernels: 34 us -> 31.7 us
    pallas_call x1, Pallas kernels: 32.5 us -> 31.1 us  [on_device(): pl.pallas_call(kernel, out_shape=pltpu.VMEM((32, ATOMS), F32), in_specs=[...]
    pallas_call x1, Pallas kernels: 1.54 us -> 0.63 us  [on_device(): pl.pallas_call(finish, out_shape=(out, out, out, out), in_specs=[vmem], o...]
where the time goes in v4:
time: 33.2 us; the launch traced here: 33 us
  Pallas kernels  31.7 us (95%)
  between operations  1.29 us (4%)
    pallas_call x1, Pallas kernels, on_device(): pl.pallas_call(kernel, out_shape=pltpu.VMEM((32, ATOMS), F32), in_specs=[...  31.1 us

profile of v4, /device:TPU:1, one launch (start us, length us, event | category | flops | bytes accessed | tf_op | source)
XLA Modules:
  0.0 33.0 jit_solution(2914715792846859974)
XLA Ops:
  1.3 31.1 %outer_step.1.packed = f32[32,1024]{1,0:T(8,128)S(1)} custom-call(f32[3,1024]{1,0:T(4,128)} %refs_0_.1, f32[3,1024]{1,0:T(4,128)} %refs_1_.1, f32[1,1024]{1,0:T(1,128)} %bitcast.7, f32[1,1024]{1,0:T(1,128)} %bitcast.8, f32[3,1024]{1,0:T(4,128)} %refs_4_.1, f32[3,1024]{1,0:T(4,128)} %refs_5_.1, s32[2,1024]{1,0:T(2,128)} %refs_6_.1, f32[1,1024]{1,0:T(1,128)} %bitcast.9, ...), custom_call_target="tpu_custom_call" | custom-call | tf_op jit(solution)/shard_map/outer_step/pallas_call | solution.py:419
  32.4 0.6 %finish.1 = (f32[3,1024]{1,0:T(4,128)}, f32[3,1024]{1,0:T(4,128)}, f32[3,1024]{1,0:T(4,128)}, f32[3,1024]{1,0:T(4,128)}) custom-call(f32[32,1024]{1,0:T(8,128)S(1)} %outer_step.1.packed), custom_call_target="tpu_custom_call" | custom-call | tf_op jit(solution)/shard_map/finish/pallas_call | solution.py:447

commit v5 on v4

--- a/solution.py
+++ b/solution.py
@@ -182,14 +182,15 @@
         assert not beside
         return tuple(acc)
 
-    def chosen(source, index):
+    def chosen(packed, index):
         low = jnp.broadcast_to(index & (TILE - 1), (8, TILE))
         tile = jnp.broadcast_to(index >> 7, (8, TILE))
         out = jnp.zeros((8, TILE), F32)
-        for t in range(OWN_TILES):
-            cols = source[:, t * TILE : (t + 1) * TILE]
-            out = jnp.where(tile == t, jnp.take_along_axis(cols, low, axis=1, mode="promise_in_bounds"), out)
-        return out
+        for t in range(OWN_TILES // 2):
+            cols = packed[:, t * TILE : (t + 1) * TILE]
+            found = jnp.take_along_axis(cols, low, axis=1, mode="promise_in_bounds")
+            out = jnp.where((tile & 3) == t, found, out)
+        return jnp.where(tile[0:4] < OWN_TILES // 2, out[0:4], out[4:8])
 
     def advance():
         v = v_ref[...] + (0.5 * STEP) * mass * f_ref[...]
@@ -199,10 +200,11 @@
         return jnp.where(row == 3, charge[...], x)
 
     def export(k, source):
+        packed = jnp.concatenate([source[0:4, : ATOMS // 2], source[0:4, ATOMS // 2 :]], axis=0)
         for face in range(FACES):
             for part in range(HALO // TILE):
                 cols = slice(part * TILE, (part + 1) * TILE)
-                send[k, face, :, cols] = chosen(source, halo[face : face + 1, cols])[0:4, :]
+                send[k, face, :, cols] = chosen(packed, halo[face : face + 1, cols])
 
     def gathered(acc, x):
         parts = []

time: 33.2 us -> 33.1 us (level)
  no operation moved by 1% of the time
where the time goes in v5:
time: 33.1 us; the launch traced here: 32.9 us
  Pallas kernels  31.6 us (95%)
  between operations  1.29 us (4%)
    pallas_call x1, Pallas kernels, on_device(): pl.pallas_call(kernel, out_shape=pltpu.VMEM((32, ATOMS), F32), in_specs=[...  31 us

profile of v5, /device:TPU:1, one launch (start us, length us, event | category | flops | bytes accessed | tf_op | source)
XLA Modules:
  0.0 32.9 jit_solution(10584685759005509385)
XLA Ops:
  1.3 31.0 %outer_step.1.packed = f32[32,1024]{1,0:T(8,128)S(1)} custom-call(f32[3,1024]{1,0:T(4,128)} %refs_0_.1, f32[3,1024]{1,0:T(4,128)} %refs_1_.1, f32[1,1024]{1,0:T(1,128)} %bitcast.7, f32[1,1024]{1,0:T(1,128)} %bitcast.8, f32[3,1024]{1,0:T(4,128)} %refs_4_.1, f32[3,1024]{1,0:T(4,128)} %refs_5_.1, s32[2,1024]{1,0:T(2,128)} %refs_6_.1, f32[1,1024]{1,0:T(1,128)} %bitcast.9, ...), custom_call_target="tpu_custom_call" | custom-call | tf_op jit(solution)/shard_map/outer_step/pallas_call | solution.py:421
  32.3 0.6 %finish.1 = (f32[3,1024]{1,0:T(4,128)}, f32[3,1024]{1,0:T(4,128)}, f32[3,1024]{1,0:T(4,128)}, f32[3,1024]{1,0:T(4,128)}) custom-call(f32[32,1024]{1,0:T(8,128)S(1)} %outer_step.1.packed), custom_call_target="tpu_custom_call" | custom-call | tf_op jit(solution)/shard_map/finish/pallas_call | solution.py:449
